TPU v7x, 32 devices: a whole 2x2x4 slice. The times are simulated.
32 devices in a mesh: dp: 8 (over y, x, core), tensor: 4 (over z).
Axes of the slice: x: 2, y: 2, z: 4, core: 2. Of those that a mesh axis runs over, the one named last changes fastest.
Arguments:
- hidden_in: bfloat16 [8192, 2048], P(('dp', 'tensor')), may hold values from -6 to 6
- query_proj: bfloat16 [2048, 2048], P('dp', 'tensor'), may hold values from -0.125 to 0.125
- key_proj: bfloat16 [2048, 1024], P('dp', 'tensor'), may hold values from -0.125 to 0.125
- value_proj: bfloat16 [2048, 1024], P('dp', 'tensor'), may hold values from -0.125 to 0.125
- out_proj: bfloat16 [2048, 2048], P('tensor', 'dp'), may hold values from -1 to 1
- gate_proj: bfloat16 [2048, 6144], P('dp', 'tensor'), may hold values from -0.125 to 0.125
- up_proj: bfloat16 [2048, 6144], P('dp', 'tensor'), may hold values from -0.125 to 0.125
- down_proj: bfloat16 [6144, 2048], P('tensor', 'dp'), may hold values from -0.078125 to 0.078125
- attn_norm: float32 [2048], replicated, may hold values from 0.25 to 1.75
- query_norm: float32 [128], replicated, may hold values from 0.25 to 1.75
- key_norm: float32 [128], replicated, may hold values from 0.25 to 1.75
- ffn_norm: float32 [2048], replicated, may hold values from 0.25 to 1.75
- cotangent: bfloat16 [8192, 2048], P(('dp', 'tensor')), may hold values from -6 to 6
Outputs:
- hidden_out: bfloat16 [8192, 2048], P(('dp', 'tensor'))
- dhidden_in: bfloat16 [8192, 2048], P(('dp', 'tensor'))
- dquery_proj: float32 [2048, 2048], P('dp', 'tensor')
- dkey_proj: float32 [2048, 1024], P('dp', 'tensor')
- dvalue_proj: float32 [2048, 1024], P('dp', 'tensor')
- dout_proj: float32 [2048, 2048], P('tensor', 'dp')
- dgate_proj: float32 [2048, 6144], P('dp', 'tensor')
- dup_proj: float32 [2048, 6144], P('dp', 'tensor')
- ddown_proj: float32 [6144, 2048], P('tensor', 'dp')
- dattn_norm: float32 [2048], replicated
- dquery_norm: float32 [128], replicated
- dkey_norm: float32 [128], replicated
- dffn_norm: float32 [2048], replicated
All inputs are finite; a program needn't handle non-finite values.
Results may differ from a plain program's by a relative error of at most 0.022.
Values may be sent and summed in bfloat16 or wider, within the bound.
A program may use at most 256 MiB of HBM per device.

v0:
```python
import math

import jax
import jax.numpy as jnp
from jax import lax
from jax.sharding import PartitionSpec as P

HEAD_DIM = 128
SEQ_LEN = 1024


EPSILON = 1e-06
ROPE_BASE = 1000000.0
NEG_FILL = -1e30


def norm_forward(values, gain):
    inverse = lax.rsqrt(jnp.mean(values * values, axis=-1, keepdims=True) + EPSILON)
    unit_vals = values * inverse
    return (unit_vals * gain, unit_vals, inverse)


def norm_backward(grad_normed, unit_vals, inverse, gain):
    grad_unit = grad_normed * gain
    grad_values = inverse * (
        grad_unit - unit_vals * jnp.mean(grad_unit * unit_vals, axis=-1, keepdims=True)
    )
    grad_gain = jnp.sum((grad_normed * unit_vals).reshape(-1, gain.shape[0]), axis=0)
    return (grad_values, grad_gain)


def rope_tables(positions, width):
    half_width = width // 2
    freqs = ROPE_BASE ** (-(jnp.arange(half_width, dtype=jnp.float32) * (2.0 / width)))
    angles = positions.astype(jnp.float32)[:, None] * freqs[None, :]
    angles = jnp.concatenate([angles, angles], axis=1)
    return (jnp.cos(angles), jnp.sin(angles))


def rotate_half(values):
    half_width = values.shape[-1] // 2
    return jnp.concatenate([-values[..., half_width:], values[..., :half_width]], axis=-1)


def rotate_back(values):
    half_width = values.shape[-1] // 2
    return jnp.concatenate([values[..., half_width:], -values[..., :half_width]], axis=-1)


def masked_scores(query_part, key_rot, offset, score_scale):
    length = key_rot.shape[0]
    q_block = query_part.shape[0]
    scores = (
        jnp.einsum("qkgd,tkd->kgqt", query_part, key_rot, preferred_element_type=jnp.float32)
        * score_scale
    )
    query_pos = offset + jnp.arange(q_block)
    key_pos = jnp.arange(length)
    return jnp.where(key_pos[None, :] <= query_pos[:, None], scores, NEG_FILL)


def attend_forward(query_rot, key_rot, values_bf, score_scale):
    length = query_rot.shape[0]
    q_block = min(512, length)
    attended_parts = []
    total_parts = []
    for offset in range(0, length, q_block):
        scores = masked_scores(query_rot[offset : offset + q_block], key_rot, offset, score_scale)
        top_score = jnp.max(scores, axis=-1, keepdims=True)
        log_total = top_score + jnp.log(
            jnp.sum(jnp.exp(scores - top_score), axis=-1, keepdims=True)
        )
        probs_bf = jnp.exp(scores - log_total).astype(jnp.bfloat16)
        attended_parts.append(
            jnp.einsum(
                "kgqt,tkd->qkgd", probs_bf, values_bf, preferred_element_type=jnp.float32
            ).astype(jnp.bfloat16)
        )
        total_parts.append(log_total)
    return (jnp.concatenate(attended_parts, axis=0), jnp.concatenate(total_parts, axis=2))


def attend_backward(query_rot, key_rot, values_bf, attended, grad_attended, log_total, score_scale):
    length = query_rot.shape[0]
    q_block = min(512, length)
    grad_keys = jnp.zeros(key_rot.shape, jnp.float32)
    grad_vals = jnp.zeros(values_bf.shape, jnp.float32)
    query_parts = []
    for offset in range(0, length, q_block):
        query_part = query_rot[offset : offset + q_block]
        grad_part = grad_attended[offset : offset + q_block]
        scores = masked_scores(query_part, key_rot, offset, score_scale)
        prob_vals = jnp.exp(scores - log_total[:, :, offset : offset + q_block])
        grad_vals = grad_vals + jnp.einsum(
            "kgqt,qkgd->tkd",
            prob_vals.astype(jnp.bfloat16),
            grad_part,
            preferred_element_type=jnp.float32,
        )
        grad_probs = jnp.einsum(
            "qkgd,tkd->kgqt", grad_part, values_bf, preferred_element_type=jnp.float32
        )
        delta = jnp.sum(
            grad_part.astype(jnp.float32) * attended[offset : offset + q_block].astype(jnp.float32),
            axis=-1,
        )
        delta = jnp.transpose(delta, (1, 2, 0))[..., None]
        grad_scores = (prob_vals * (grad_probs - delta) * score_scale).astype(jnp.bfloat16)
        query_parts.append(
            jnp.einsum("kgqt,tkd->qkgd", grad_scores, key_rot, preferred_element_type=jnp.float32)
        )
        grad_keys = grad_keys + jnp.einsum(
            "kgqt,qkgd->tkd", grad_scores, query_part, preferred_element_type=jnp.float32
        )
    return (jnp.concatenate(query_parts, axis=0), grad_keys, grad_vals)


def per_device(
    hidden_in,
    query_proj,
    key_proj,
    value_proj,
    out_proj,
    gate_proj,
    up_proj,
    down_proj,
    attn_norm,
    query_norm,
    key_norm,
    ffn_norm,
    cotangent,
):
    query_full, key_full, value_full, gate_full, up_full = (
        lax.all_gather(query_proj, "dp", axis=0, tiled=True),
        lax.all_gather(key_proj, "dp", axis=0, tiled=True),
        lax.all_gather(value_proj, "dp", axis=0, tiled=True),
        lax.all_gather(gate_proj, "dp", axis=0, tiled=True),
        lax.all_gather(up_proj, "dp", axis=0, tiled=True),
    )
    out_full, down_full = (
        lax.all_gather(out_proj, "dp", axis=1, tiled=True),
        lax.all_gather(down_proj, "dp", axis=1, tiled=True),
    )
    local_rows = hidden_in.shape[0]
    score_scale = 1.0 / math.sqrt(HEAD_DIM)
    inputs = hidden_in.astype(jnp.float32)
    normed, unit_one, inv_one = norm_forward(inputs, attn_norm)
    normed_bf = lax.all_gather(normed.astype(jnp.bfloat16), "tensor", axis=0, tiled=True)
    group_rows = normed_bf.shape[0]
    local_heads = query_full.shape[1] // HEAD_DIM
    local_kv = key_full.shape[1] // HEAD_DIM
    groups = local_heads // local_kv
    sequences = group_rows // SEQ_LEN
    queries = jnp.dot(normed_bf, query_full, preferred_element_type=jnp.float32).reshape(
        group_rows, local_heads, HEAD_DIM
    )
    keys_raw = jnp.dot(normed_bf, key_full, preferred_element_type=jnp.float32).reshape(
        group_rows, local_kv, HEAD_DIM
    )
    values_bf = jnp.dot(normed_bf, value_full, preferred_element_type=jnp.float32).astype(
        jnp.bfloat16
    )
    values_bf = values_bf.reshape(sequences, SEQ_LEN, local_kv, HEAD_DIM)
    query_normed, query_unit, query_inv = norm_forward(queries, query_norm)
    key_normed, key_unit, key_inv = norm_forward(keys_raw, key_norm)
    cosine_table, sine_table = rope_tables(jnp.arange(group_rows) % SEQ_LEN, HEAD_DIM)
    cosine_table = cosine_table[:, None, :]
    sine_table = sine_table[:, None, :]
    query_rot = (query_normed * cosine_table + rotate_half(query_normed) * sine_table).astype(
        jnp.bfloat16
    )
    query_rot = query_rot.reshape(sequences, SEQ_LEN, local_kv, groups, HEAD_DIM)
    key_rot = (key_normed * cosine_table + rotate_half(key_normed) * sine_table).astype(
        jnp.bfloat16
    )
    key_rot = key_rot.reshape(sequences, SEQ_LEN, local_kv, HEAD_DIM)
    attended, log_total = lax.map(
        lambda packed: attend_forward(packed[0], packed[1], packed[2], score_scale),
        (query_rot, key_rot, values_bf),
    )
    attended_flat = attended.reshape(group_rows, local_heads * HEAD_DIM)
    rows_part = lax.slice_in_dim(attended_flat, 0, lax.axis_size("tensor") * local_rows, axis=0)
    residual_mid = inputs + lax.psum_scatter(
        jnp.dot(rows_part, out_full, preferred_element_type=jnp.float32).astype(jnp.bfloat16),
        "tensor",
        scatter_dimension=0,
        tiled=True,
    ).astype(jnp.float32)
    ffn_normed, unit_two, inv_two = norm_forward(residual_mid, ffn_norm)
    ffn_in = lax.all_gather(ffn_normed.astype(jnp.bfloat16), "tensor", axis=0, tiled=True)
    gate_vals = jnp.dot(ffn_in, gate_full, preferred_element_type=jnp.float32)
    up_vals = jnp.dot(ffn_in, up_full, preferred_element_type=jnp.float32)
    sigmoid_gate = jax.nn.sigmoid(gate_vals)
    hidden_act = (gate_vals * sigmoid_gate * up_vals).astype(jnp.bfloat16)
    rows_part = lax.slice_in_dim(hidden_act, 0, lax.axis_size("tensor") * local_rows, axis=0)
    hidden_out = (
        residual_mid
        + lax.psum_scatter(
            jnp.dot(rows_part, down_full, preferred_element_type=jnp.float32).astype(jnp.bfloat16),
            "tensor",
            scatter_dimension=0,
            tiled=True,
        ).astype(jnp.float32)
    ).astype(jnp.bfloat16)
    cot_full = lax.all_gather(cotangent, "tensor", axis=0, tiled=True)
    grad_hidden = jnp.dot(cot_full, down_full.T, preferred_element_type=jnp.float32)
    down_grad = jnp.dot(hidden_act.T, cot_full, preferred_element_type=jnp.float32)
    grad_up = (grad_hidden * (gate_vals * sigmoid_gate)).astype(jnp.bfloat16)
    grad_gate = (
        grad_hidden * up_vals * sigmoid_gate * (1.0 + gate_vals * (1.0 - sigmoid_gate))
    ).astype(jnp.bfloat16)
    gate_grad = jnp.dot(ffn_in.T, grad_gate, preferred_element_type=jnp.float32)
    up_grad = jnp.dot(ffn_in.T, grad_up, preferred_element_type=jnp.float32)
    gate_part = lax.slice_in_dim(grad_gate, 0, lax.axis_size("tensor") * local_rows, axis=0)
    up_part = lax.slice_in_dim(grad_up, 0, lax.axis_size("tensor") * local_rows, axis=0)
    total = jnp.dot(gate_part, gate_full.T, preferred_element_type=jnp.float32)
    grad_ffn_in = lax.psum_scatter(
        (total + jnp.dot(up_part, up_full.T, preferred_element_type=jnp.float32)).astype(
            jnp.bfloat16
        ),
        "tensor",
        scatter_dimension=0,
        tiled=True,
    ).astype(jnp.float32)
    grad_part, ffn_gain_grad = norm_backward(grad_ffn_in, unit_two, inv_two, ffn_norm)
    grad_mid = cotangent.astype(jnp.float32) + grad_part
    grad_mid_bf = lax.all_gather(grad_mid.astype(jnp.bfloat16), "tensor", axis=0, tiled=True)
    out_grad = jnp.dot(attended_flat.T, grad_mid_bf, preferred_element_type=jnp.float32)
    grad_attended = jnp.dot(grad_mid_bf, out_full.T, preferred_element_type=jnp.float32).astype(
        jnp.bfloat16
    )
    grad_attended = grad_attended.reshape(sequences, SEQ_LEN, local_kv, groups, HEAD_DIM)
    grad_query_rot, grad_key_rot, grad_vals = lax.map(
        lambda packed: attend_backward(
            packed[0], packed[1], packed[2], packed[3], packed[4], packed[5], score_scale
        ),
        (query_rot, key_rot, values_bf, attended, grad_attended, log_total),
    )
    grad_query_rot = grad_query_rot.reshape(group_rows, local_heads, HEAD_DIM)
    grad_key_rot = grad_key_rot.reshape(group_rows, local_kv, HEAD_DIM)
    grad_query_normed = grad_query_rot * cosine_table + rotate_back(grad_query_rot * sine_table)
    grad_key_normed = grad_key_rot * cosine_table + rotate_back(grad_key_rot * sine_table)
    grad_queries, query_gain_grad = norm_backward(
        grad_query_normed, query_unit, query_inv, query_norm
    )
    grad_keys, key_gain_grad = norm_backward(grad_key_normed, key_unit, key_inv, key_norm)
    grad_queries_bf = grad_queries.reshape(group_rows, local_heads * HEAD_DIM).astype(jnp.bfloat16)
    grad_keys_bf = grad_keys.reshape(group_rows, local_kv * HEAD_DIM).astype(jnp.bfloat16)
    grad_vals_bf = grad_vals.reshape(group_rows, local_kv * HEAD_DIM).astype(jnp.bfloat16)
    query_grad = jnp.dot(normed_bf.T, grad_queries_bf, preferred_element_type=jnp.float32)
    key_grad = jnp.dot(normed_bf.T, grad_keys_bf, preferred_element_type=jnp.float32)
    value_grad = jnp.dot(normed_bf.T, grad_vals_bf, preferred_element_type=jnp.float32)
    value_part = lax.slice_in_dim(grad_vals_bf, 0, lax.axis_size("tensor") * local_rows, axis=0)
    total = jnp.dot(grad_queries_bf, query_full.T, preferred_element_type=jnp.float32)
    total = total + jnp.dot(grad_keys_bf, key_full.T, preferred_element_type=jnp.float32)
    grad_normed_in = lax.psum_scatter(
        (total + jnp.dot(value_part, value_full.T, preferred_element_type=jnp.float32)).astype(
            jnp.bfloat16
        ),
        "tensor",
        scatter_dimension=0,
        tiled=True,
    ).astype(jnp.float32)
    grad_first, attn_gain_grad = norm_backward(grad_normed_in, unit_one, inv_one, attn_norm)
    dhidden_in = (grad_mid + grad_first).astype(jnp.bfloat16)
    gain_totals = lax.psum(
        (attn_gain_grad, query_gain_grad, key_gain_grad, ffn_gain_grad), ("dp", "tensor")
    )
    weight_sums = (
        lax.psum_scatter(
            query_grad.astype(jnp.bfloat16), "dp", scatter_dimension=0, tiled=True
        ).astype(jnp.float32),
        lax.psum_scatter(
            key_grad.astype(jnp.bfloat16), "dp", scatter_dimension=0, tiled=True
        ).astype(jnp.float32),
        lax.psum_scatter(
            value_grad.astype(jnp.bfloat16), "dp", scatter_dimension=0, tiled=True
        ).astype(jnp.float32),
        lax.psum_scatter(
            out_grad.astype(jnp.bfloat16), "dp", scatter_dimension=1, tiled=True
        ).astype(jnp.float32),
        lax.psum_scatter(
            gate_grad.astype(jnp.bfloat16), "dp", scatter_dimension=0, tiled=True
        ).astype(jnp.float32),
        lax.psum_scatter(
            up_grad.astype(jnp.bfloat16), "dp", scatter_dimension=0, tiled=True
        ).astype(jnp.float32),
        lax.psum_scatter(
            down_grad.astype(jnp.bfloat16), "dp", scatter_dimension=1, tiled=True
        ).astype(jnp.float32),
    )
    return (
        hidden_out,
        dhidden_in,
        weight_sums[0],
        weight_sums[1],
        weight_sums[2],
        weight_sums[3],
        weight_sums[4],
        weight_sums[5],
        weight_sums[6],
        gain_totals[0],
        gain_totals[1],
        gain_totals[2],
        gain_totals[3],
    )


def solution(mesh):
    placed = (
        P(("dp", "tensor"), None),
        P("dp", "tensor"),
        P("dp", "tensor"),
        P("dp", "tensor"),
        P("tensor", "dp"),
        P("dp", "tensor"),
        P("dp", "tensor"),
        P("tensor", "dp"),
        P(),
        P(),
        P(),
        P(),
        P(("dp", "tensor"), None),
    )
    return jax.shard_map(
        per_device,
        mesh=mesh,
        in_specs=placed,
        out_specs=(
            P(("dp", "tensor"), None),
            P(("dp", "tensor"), None),
            P("dp", "tensor"),
            P("dp", "tensor"),
            P("dp", "tensor"),
            P("tensor", "dp"),
            P("dp", "tensor"),
            P("dp", "tensor"),
            P("tensor", "dp"),
            P(),
            P(),
            P(),
            P(),
        ),
        check_vma=False,
    )
```

profile of v0, /device:TPU:9, one launch (start us, length us, event | category | flops | bytes accessed | tf_op | source)
XLA Modules:
  0.0 1320.6 jit_solution(17991608183224586273)
XLA Ops:
  16.6 18.3 %all-gather.16.cloned.1.call-done = bf16[2048,256]{1,0:T(8,128)(2,1)} async-done(((bf16[256,256]{1,0:T(8,128)(2,1)}), bf16[2048,256]{1,0:T(8,128)(2,1)}) %all-gather.16.cloned.1.call-update) | async-done | bytes 1048592 | tf_op jit(solution)/shard_map/all_gather | solution.py:135
  34.8 79.9 %all-gather.12.cloned.1.call-done = bf16[1024,2048]{1,0:T(8,128)(2,1)} async-done(((bf16[256,2048]{1,0:T(8,128)(2,1)}), bf16[1024,2048]{1,0:T(8,128)(2,1)}) %all-gather.12.cloned.1.call-update) | async-done | bytes 4194320 | tf_op jit(solution)/shard_map/all_gather | solution.py:148
  119.8 26.1 %all-gather.18.cloned.1.call-done = bf16[2048,512]{1,0:T(8,128)(2,1)} async-done(((bf16[256,512]{1,0:T(8,128)(2,1)}), bf16[2048,512]{1,0:T(8,128)(2,1)}) %all-gather.18.cloned.1.call-update) | async-done | bytes 2097168 | tf_op jit(solution)/shard_map/all_gather | solution.py:134
  183.7 17.3 %all-gather.20.cloned.1.call-done = bf16[512,2048]{1,0:T(8,128)(2,1)} async-done(((bf16[512,256]{1,0:T(8,128)(2,1)}), bf16[512,2048]{1,0:T(8,128)(2,1)}) %all-gather.20.cloned.1.call-update) | async-done | bytes 2097168 | tf_op jit(solution)/shard_map/all_gather | solution.py:141
  207.8 75.7 %reduce-scatter.12.cloned.1.call-done = bf16[256,2048]{1,0:T(8,128)(2,1)} async-done(((bf16[1024,2048]{1,0:T(8,128)(2,1)}), bf16[256,2048]{1,0:T(8,128)(2,1)}) %reduce-scatter.12.cloned.1.call-update) | async-done | bytes 1048592 | tf_op jit(solution)/shard_map/reduce_scatter | solution.py:183
  289.8 41.9 %all-gather.24.cloned.1.call-done = bf16[2048,1536]{1,0:T(8,128)(2,1)} async-done(((bf16[256,1536]{1,0:T(8,128)(2,1)}), bf16[2048,1536]{1,0:T(8,128)(2,1)}) %all-gather.24.cloned.1.call-update) | async-done | bytes 6291472 | tf_op jit(solution)/shard_map/all_gather | solution.py:137
  331.7 79.9 %all-gather.22.cloned.1.call-done = bf16[1024,2048]{1,0:T(8,128)(2,1)} async-done(((bf16[256,2048]{1,0:T(8,128)(2,1)}), bf16[1024,2048]{1,0:T(8,128)(2,1)}) %all-gather.22.cloned.1.call-update) | async-done | bytes 4194320 | tf_op jit(solution)/shard_map/all_gather | solution.py:190
  411.6 11.9 fusion.63
  423.5 37.0 %all-gather.26.cloned.1.call-done = bf16[2048,1536]{1,0:T(8,128)(2,1)} async-done(((bf16[256,1536]{1,0:T(8,128)(2,1)}), bf16[2048,1536]{1,0:T(8,128)(2,1)}) %all-gather.26.cloned.1.call-update) | async-done | bytes 6291472 | tf_op jit(solution)/shard_map/all_gather | solution.py:138
  472.1 67.4 %all-gather.30.cloned.1.call-done = bf16[1024,2048]{1,0:T(8,128)(2,1)} async-done(((bf16[256,2048]{1,0:T(8,128)(2,1)}), bf16[1024,2048]{1,0:T(8,128)(2,1)}) %all-gather.30.cloned.1.call-update) | async-done | bytes 4194320 | tf_op jit(solution)/shard_map/all_gather | solution.py:205
  539.6 50.0 %all-gather.28.cloned.1.call-done = bf16[1536,2048]{1,0:T(8,128)(2,1)} async-done(((bf16[1536,256]{1,0:T(8,128)(2,1)}), bf16[1536,2048]{1,0:T(8,128)(2,1)}) %all-gather.28.cloned.1.call-update) | async-done | bytes 6291472 | tf_op jit(solution)/shard_map/all_gather | solution.py:142
  589.6 16.0 %multiply_convert_fusion = (bf16[1024,1536]{1,0:T(8,128)(2,1)S(1)}, bf16[1024,1536]{1,0:T(8,128)(2,1)S(1)}, bf16[1024,1536]{1,0:T(8,128)(2,1)}) fusion(f32[1024,1536]{1,0:T(8,128)} %fusion.63, f32[1024,1536]{1,0:T(8,128)} %fusion.64, bf16[1024,2048]{1,0:T(8,128)(2,1)} %all-gather.30.cloned.1.call-done, bf16[1536,2048]{1,0:T(8,128)(2,1)} %all-gather.28.cloned.1.call-done), kind=kOutput, calls=%fused_computation.21 | convolution fusion | flops 6466043904 | bytes 32505856 | tf_op jit(solution)/shard_map/dot_general | solution.py:206
  625.5 76.4 %reduce-scatter.16.cloned.1.call-done = bf16[256,2048]{1,0:T(8,128)(2,1)} async-done(((bf16[1024,2048]{1,0:T(8,128)(2,1)}), bf16[256,2048]{1,0:T(8,128)(2,1)}) %reduce-scatter.16.cloned.1.call-update) | async-done | bytes 1048592 | tf_op jit(solution)/shard_map/reduce_scatter | solution.py:217
  742.1 44.1 %all-gather.32.cloned.1.call-done = bf16[1024,2048]{1,0:T(8,128)(2,1)} async-done(((bf16[256,2048]{1,0:T(8,128)(2,1)}), bf16[1024,2048]{1,0:T(8,128)(2,1)}) %all-gather.32.cloned.1.call-update) | async-done | bytes 4194320 | tf_op jit(solution)/shard_map/all_gather | solution.py:227
  863.5 12.0 convolution_convert_fusion.3
  878.1 39.1 %reduce-scatter.30.cloned.1.call-done = bf16[256,1536]{1,0:T(8,128)(2,1)} async-done(((bf16[2048,1536]{1,0:T(8,128)(2,1)}), bf16[256,1536]{1,0:T(8,128)(2,1)}) %reduce-scatter.30.cloned.1.call-update) | async-done | bytes 786448 | tf_op jit(solution)/shard_map/reduce_scatter | solution.py:285
  919.6 62.4 %reduce-scatter.32.cloned.1.call-done = bf16[1536,256]{1,0:T(8,128)(2,1)} async-done(((bf16[1536,2048]{1,0:T(8,128)(2,1)}), bf16[1536,256]{1,0:T(8,128)(2,1)}) %reduce-scatter.32.cloned.1.call-update) | async-done | bytes 786448 | tf_op jit(solution)/shard_map/reduce_scatter | solution.py:288
  984.5 36.4 %reduce-scatter.24.cloned.1.call-done = bf16[256,256]{1,0:T(8,128)(2,1)} async-done(((bf16[2048,256]{1,0:T(8,128)(2,1)}), bf16[256,256]{1,0:T(8,128)(2,1)}) %reduce-scatter.24.cloned.1.call-update) | async-done | bytes 131088 | tf_op jit(solution)/shard_map/reduce_scatter | solution.py:276
  1022.5 37.4 %reduce-scatter.22.cloned.1.call-done = bf16[256,256]{1,0:T(8,128)(2,1)} async-done(((bf16[2048,256]{1,0:T(8,128)(2,1)}), bf16[256,256]{1,0:T(8,128)(2,1)}) %reduce-scatter.22.cloned.1.call-update) | async-done | bytes 131088 | tf_op jit(solution)/shard_map/reduce_scatter | solution.py:273
  1061.5 43.0 %reduce-scatter.26.cloned.1.call-done = bf16[512,256]{1,0:T(8,128)(2,1)} async-done(((bf16[512,2048]{1,0:T(8,128)(2,1)}), bf16[512,256]{1,0:T(8,128)(2,1)}) %reduce-scatter.26.cloned.1.call-update) | async-done | bytes 262160 | tf_op jit(solution)/shard_map/reduce_scatter | solution.py:279
  1106.3 42.5 %reduce-scatter.20.cloned.1.call-done = bf16[256,512]{1,0:T(8,128)(2,1)} async-done(((bf16[2048,512]{1,0:T(8,128)(2,1)}), bf16[256,512]{1,0:T(8,128)(2,1)}) %reduce-scatter.20.cloned.1.call-update) | async-done | bytes 262160 | tf_op jit(solution)/shard_map/reduce_scatter | solution.py:270
  1150.6 77.4 %reduce-scatter.18.cloned.1.call-done = bf16[256,2048]{1,0:T(8,128)(2,1)} async-done(((bf16[1024,2048]{1,0:T(8,128)(2,1)}), bf16[256,2048]{1,0:T(8,128)(2,1)}) %reduce-scatter.18.cloned.1.call-update) | async-done | bytes 1048592 | tf_op jit(solution)/shard_map/reduce_scatter | solution.py:256
  1230.0 46.3 %all-reduce = (f32[2048]{0:T(1024)}, f32[128]{0:T(128)}, f32[128]{0:T(128)}, f32[2048]{0:T(1024)}) all-reduce(f32[2048]{0:T(1024)S(1)} %get-tuple-element.53, f32[128]{0:T(128)S(1)} %reduce_sum.170, f32[128]{0:T(128)S(1)} %get-tuple-element.65, f32[2048]{0:T(1024)S(1)} %get-tuple-element.51), channel_id=1, replica_groups=mesh['dp'=8,'tensor'=4] {'dp','tensor'}, use_global_device_ids=true, to_apply=%region_26.27 | all-reduce | flops 4352 | bytes 34816 | tf_op jit(solution)/shard_map/psum | solution.py:266
  1276.3 32.3 %reduce-scatter.14.cloned.1.call-done = bf16[256,2048]{1,0:T(8,128)(2,1)} async-done(((bf16[1024,2048]{1,0:T(8,128)(2,1)}), bf16[256,2048]{1,0:T(8,128)(2,1)}) %reduce-scatter.14.cloned.1.call-update) | async-done | bytes 1048592 | tf_op jit(solution)/shard_map/reduce_scatter | solution.py:198
  (294 shorter events, 234.4 us)
Async XLA Ops:
  7.2 27.7 %all-gather.16.cloned.1.call-start = ((), (), s32[]{:S(2)}) async-start(), calls=%async_computation.13 | async-start | bytes 1179648 | tf_op jit(solution)/shard_map/all_gather | solution.py:135
  7.9 106.8 %all-gather.12.cloned.1.call-start = ((), (), s32[]{:S(2)}) async-start(), calls=%async_computation.11 | async-start | bytes 5242880 | tf_op jit(solution)/shard_map/all_gather | solution.py:148
  12.0 133.9 %all-gather.18.cloned.1.call-start = ((), (), s32[]{:S(2)}) async-start(), calls=%async_computation.14 | async-start | bytes 2359296 | tf_op jit(solution)/shard_map/all_gather | solution.py:134
  12.8 158.3 %all-gather.14.cloned.1.call-start = ((), (), s32[]{:S(2)}) async-start(), calls=%async_computation.12 | async-start | bytes 1179648 | tf_op jit(solution)/shard_map/all_gather | solution.py:136
  13.3 187.6 %all-gather.20.cloned.1.call-start = ((), (), s32[]{:S(2)}) async-start(), calls=%async_computation.15 | async-start | bytes 2359296 | tf_op jit(solution)/shard_map/all_gather | solution.py:141
  13.9 269.5 %reduce-scatter.12.cloned.1.call-start = ((), (), s32[]{:S(2)}) async-start(), calls=%async_computation.16 | async-start | bytes 5242880 | tf_op jit(solution)/shard_map/reduce_scatter | solution.py:183
  207.0 124.8 %all-gather.24.cloned.1.call-start = ((), (), s32[]{:S(2)}) async-start(), calls=%async_computation.18 | async-start | bytes 7077888 | tf_op jit(solution)/shard_map/all_gather | solution.py:137
  207.7 203.9 %all-gather.22.cloned.1.call-start = ((), (), s32[]{:S(2)}) async-start(), calls=%async_computation.17 | async-start | bytes 5242880 | tf_op jit(solution)/shard_map/all_gather | solution.py:190
  287.7 172.7 %all-gather.26.cloned.1.call-start = ((), (), s32[]{:S(2)}) async-start(), calls=%async_computation.19 | async-start | bytes 7077888 | tf_op jit(solution)/shard_map/all_gather | solution.py:138
  288.5 251.1 %all-gather.30.cloned.1.call-start = ((), (), s32[]{:S(2)}) async-start(), calls=%async_computation.22 | async-start | bytes 5242880 | tf_op jit(solution)/shard_map/all_gather | solution.py:205
  289.0 300.6 %all-gather.28.cloned.1.call-start = ((), (), s32[]{:S(2)}) async-start(), calls=%async_computation.20 | async-start | bytes 7077888 | tf_op jit(solution)/shard_map/all_gather | solution.py:142
  289.8 412.2 %reduce-scatter.16.cloned.1.call-start = ((), (), s32[]{:S(2)}) async-start(), calls=%async_computation.23 | async-start | bytes 5242880 | tf_op jit(solution)/shard_map/reduce_scatter | solution.py:217
  625.5 160.7 %all-gather.32.cloned.1.call-start = ((), (), s32[]{:S(2)}) async-start(), calls=%async_computation.24 | async-start | bytes 5242880 | tf_op jit(solution)/shard_map/all_gather | solution.py:227
  707.4 168.3 %reduce-scatter.28.cloned.1.call-start = ((), (), s32[]{:S(2)}) async-start(), calls=%async_computation.30 | async-start | bytes 7077888 | tf_op jit(solution)/shard_map/reduce_scatter | solution.py:282
  718.9 198.3 %reduce-scatter.30.cloned.1.call-start = ((), (), s32[]{:S(2)}) async-start(), calls=%async_computation.31 | async-start | bytes 7077888 | tf_op jit(solution)/shard_map/reduce_scatter | solution.py:285
  730.4 251.6 %reduce-scatter.32.cloned.1.call-start = ((), (), s32[]{:S(2)}) async-start(), calls=%async_computation.32 | async-start | bytes 7077888 | tf_op jit(solution)/shard_map/reduce_scatter | solution.py:288
  742.0 278.8 %reduce-scatter.24.cloned.1.call-start = ((), (), s32[]{:S(2)}) async-start(), calls=%async_computation.28 | async-start | bytes 1179648 | tf_op jit(solution)/shard_map/reduce_scatter | solution.py:276
  818.8 241.1 %reduce-scatter.22.cloned.1.call-start = ((), (), s32[]{:S(2)}) async-start(), calls=%async_computation.27 | async-start | bytes 1179648 | tf_op jit(solution)/shard_map/reduce_scatter | solution.py:273
  828.3 276.2 %reduce-scatter.26.cloned.1.call-start = ((), (), s32[]{:S(2)}) async-start(), calls=%async_computation.29 | async-start | bytes 2359296 | tf_op jit(solution)/shard_map/reduce_scatter | solution.py:279
  834.3 314.5 %reduce-scatter.20.cloned.1.call-start = ((), (), s32[]{:S(2)}) async-start(), calls=%async_computation.26 | async-start | bytes 2359296 | tf_op jit(solution)/shard_map/reduce_scatter | solution.py:270
  855.5 372.5 %reduce-scatter.18.cloned.1.call-start = ((), (), s32[]{:S(2)}) async-start(), calls=%async_computation.25 | async-start | bytes 5242880 | tf_op jit(solution)/shard_map/reduce_scatter | solution.py:256
  863.5 445.2 %reduce-scatter.14.cloned.1.call-start = ((), (), s32[]{:S(2)}) async-start(), calls=%async_computation.21 | async-start | bytes 5242880 | tf_op jit(solution)/shard_map/reduce_scatter | solution.py:198
  878.1 430.6 %copy-start.8 = (bf16[256,2048]{1,0:T(8,128)(2,1)S(1)}, bf16[256,2048]{1,0:T(8,128)(2,1)}, u32[]{:S(2)}) copy-start(bf16[256,2048]{1,0:T(8,128)(2,1)} %reduce-scatter.12.cloned.1.call-done) | copy-start | bytes 3145732
  878.1 430.6 %copy-start.28 = (bf16[256,2048]{1,0:T(8,128)(2,1)S(1)}, bf16[256,2048]{1,0:T(8,128)(2,1)}, u32[]{:S(2)}) copy-start(bf16[256,2048]{1,0:T(8,128)(2,1)} %param.25) | copy-start | bytes 3145732
  (77 other events, 2203.5 us)
Sparse Core Ops, SparseCore 0:
  9.9 24.9 all-gather.15
  37.0 77.6 all-gather.11
  116.6 29.2 all-gather.17
  147.7 23.3 all-gather.13
  172.8 28.1 all-gather.19
  207.1 76.3 reduce-scatter.11
  285.3 46.3 all-gather.23
  333.9 77.6 all-gather.21
  413.5 46.9 all-gather.25
  461.8 77.6 all-gather.29
  541.4 48.0 all-gather.27
  625.6 76.3 reduce-scatter.15
  707.5 78.6 all-gather.31
  789.4 62.6 reduce-scatter.27
  855.4 61.7 reduce-scatter.29
  920.4 61.5 reduce-scatter.31
  985.1 35.7 reduce-scatter.23
  1023.9 35.9 reduce-scatter.21
  1063.2 41.3 reduce-scatter.25
  1107.6 41.0 reduce-scatter.19
  1151.1 76.8 reduce-scatter.17
  1230.3 78.3 reduce-scatter.13
where the time goes:
time: 1330 us; the launch traced here: 1320 us
  waiting for transfers between devices  996 us (75%)
  matrix products  191 us (14%)
  other arithmetic  53.7 us (4%)
  blocking collectives  46.3 us (3%)
  local copies, waits for them, and re-layouts  15.7 us (1%)
  between operations  15.6 us (1%)
    all_gather x1, waiting for transfers between devices, per_device(): lax.all_gather(normed.astype(jnp.bfloat16), 'tensor', axis=0, tiled=True)  79.9 us
    all_gather x1, waiting for transfers between devices, per_device(): lax.all_gather(ffn_normed.astype(jnp.bfloat16), 'tensor', axis=0, tiled=T...  79.9 us
    reduce_scatter x1, waiting for transfers between devices, per_device(): lax.psum_scatter((total + jnp.dot(value_part, value_full.T, preferred_ele...  77.4 us
    reduce_scatter x1, waiting for transfers between devices, per_device(): lax.psum_scatter((total + jnp.dot(up_part, up_full.T, preferred_element_t...  76.4 us
    reduce_scatter x1, waiting for transfers between devices, per_device(): lax.psum_scatter(jnp.dot(rows_part, out_full, preferred_element_type=jnp....  75.7 us
    all_gather x1, waiting for transfers between devices, per_device(): cot_full = lax.all_gather(cotangent, 'tensor', axis=0, tiled=True)  67.4 us
    reduce_scatter x1, waiting for transfers between devices, per_device(): lax.psum_scatter(down_grad.astype(jnp.bfloat16), 'dp', scatter_dimension=...  62.4 us
    all_gather x1, waiting for transfers between devices, per_device(): lax.all_gather(down_proj, 'dp', axis=1, tiled=True)  50 us
  transfers between devices with their start and end apart: 22, of which 21 were waited for; matrix products, arithmetic and copies ran while one was open for 15% of the time, Pallas kernels for 0%

commit v1 on v0

--- a/solution.py
+++ b/solution.py
@@ -1,8 +1,11 @@
+import functools
 import math
 
 import jax
 import jax.numpy as jnp
 from jax import lax
+from jax.experimental import pallas as pl
+from jax.experimental.pallas import tpu as pltpu
 from jax.sharding import PartitionSpec as P
 
 HEAD_DIM = 128
@@ -115,6 +118,395 @@
     return (jnp.concatenate(query_parts, axis=0), grad_keys, grad_vals)
 
 
+MESH = pl.DeviceIdType.MESH
+VMEM_BYTES = 60 * 2**20
+
+
+def line_barrier(here, count):
+    barrier = pltpu.get_barrier_semaphore()
+
+    @pl.when(here > 0)
+    def _():
+        pl.semaphore_signal(
+            barrier, inc=1, device_id={"tensor": here - 1}, device_id_type=MESH
+        )
+
+    @pl.when(here < count - 1)
+    def _():
+        pl.semaphore_signal(
+            barrier, inc=1, device_id={"tensor": here + 1}, device_id_type=MESH
+        )
+
+    inside = jnp.logical_and(here > 0, here < count - 1)
+
+    @pl.when(inside)
+    def _():
+        pl.semaphore_wait(barrier, 2)
+
+    @pl.when(jnp.logical_not(inside))
+    def _():
+        pl.semaphore_wait(barrier, 1)
+
+
+def block_of(ref, index, rows):
+    return ref.at[pl.ds(pl.multiple_of(index * rows, rows), rows)]
+
+
+class LineGather:
+    def __init__(self, here, count, rows, full, send_right, send_left, recv):
+        self.here, self.count, self.rows = here, count, rows
+        self.full, self.send_right, self.send_left, self.recv = full, send_right, send_left, recv
+
+    def copy(self, index, step, sems, src=None):
+        block = block_of(self.full, index, self.rows)
+        return pltpu.make_async_remote_copy(
+            src_ref=block if src is None else src,
+            dst_ref=block,
+            send_sem=sems.at[index],
+            recv_sem=self.recv.at[index],
+            device_id={"tensor": self.here + step},
+            device_id_type=MESH,
+        )
+
+    def begin(self, own):
+        @pl.when(self.here < self.count - 1)
+        def _():
+            self.copy(self.here, 1, self.send_right, own).start()
+
+        @pl.when(self.here > 0)
+        def _():
+            self.copy(self.here, -1, self.send_left, own).start()
+
+    def arrive(self, hop, then):
+        here, count = self.here, self.count
+
+        @pl.when(here >= hop)
+        def _():
+            index = here - hop
+            self.copy(index, 1, self.send_right).wait_recv()
+
+            @pl.when(here < count - 1)
+            def _():
+                self.copy(index, 1, self.send_right).start()
+
+        @pl.when(here < count - hop)
+        def _():
+            index = here + hop
+            self.copy(index, -1, self.send_left).wait_recv()
+
+            @pl.when(here > 0)
+            def _():
+                self.copy(index, -1, self.send_left).start()
+
+        @pl.when(here >= hop)
+        def _():
+            then(here - hop)
+
+        @pl.when(here < count - hop)
+        def _():
+            then(here + hop)
+
+    def finish(self):
+        here, count = self.here, self.count
+        for hop in range(count):
+
+            @pl.when(jnp.logical_and(here >= hop, here < count - 1))
+            def _():
+                self.copy(here - hop, 1, self.send_right).wait_send()
+
+            @pl.when(jnp.logical_and(here < count - hop, here > 0))
+            def _():
+                self.copy(here + hop, -1, self.send_left).wait_send()
+
+
+class LineScatter:
+    def __init__(self, here, count, from_left, from_right, to_right, to_left, sems):
+        self.here, self.count = here, count
+        self.from_left, self.from_right = from_left, from_right
+        self.to_right, self.to_left = to_right, to_left
+        self.sems = sems
+
+    def right(self, index):
+        return pltpu.make_async_remote_copy(
+            src_ref=self.to_right.at[index],
+            dst_ref=self.from_left.at[index],
+            send_sem=self.sems.at[0, index],
+            recv_sem=self.sems.at[1, index],
+            device_id={"tensor": self.here + 1},
+            device_id_type=MESH,
+        )
+
+    def left(self, index):
+        return pltpu.make_async_remote_copy(
+            src_ref=self.to_left.at[index],
+            dst_ref=self.from_right.at[index],
+            send_sem=self.sems.at[2, index],
+            recv_sem=self.sems.at[3, index],
+            device_id={"tensor": self.here - 1},
+            device_id_type=MESH,
+        )
+
+    def step(self, hop, part):
+        here, count = self.here, self.count
+
+        @pl.when(jnp.logical_and(hop >= here, here < count - 1))
+        def _():
+            index = count - 1 + here - hop
+
+            @pl.when(here > 0)
+            def _():
+                self.right(index).wait_recv()
+                self.to_right[index] = (
+                    part(index).astype(jnp.float32)
+                    + self.from_left[index].astype(jnp.float32)
+                ).astype(jnp.bfloat16)
+
+            @pl.when(here == 0)
+            def _():
+                self.to_right[index] = part(index)
+
+            self.right(index).start()
+
+        @pl.when(jnp.logical_and(hop >= count - 1 - here, here > 0))
+        def _():
+            index = hop + here + 1 - count
+
+            @pl.when(here < count - 1)
+            def _():
+                self.left(index).wait_recv()
+                self.to_left[index] = (
+                    part(index).astype(jnp.float32)
+                    + self.from_right[index].astype(jnp.float32)
+                ).astype(jnp.bfloat16)
+
+            @pl.when(here == count - 1)
+            def _():
+                self.to_left[index] = part(index)
+
+            self.left(index).start()
+
+    def finish(self, own, store):
+        here, count = self.here, self.count
+
+        @pl.when(here > 0)
+        def _():
+            self.right(here).wait_recv()
+
+        @pl.when(here < count - 1)
+        def _():
+            self.left(here).wait_recv()
+
+        @pl.when(here == 0)
+        def _():
+            store(own() + self.from_right[here].astype(jnp.float32))
+
+        @pl.when(here == count - 1)
+        def _():
+            store(own() + self.from_left[here].astype(jnp.float32))
+
+        @pl.when(jnp.logical_and(here > 0, here < count - 1))
+        def _():
+            store(
+                own()
+                + self.from_left[here].astype(jnp.float32)
+                + self.from_right[here].astype(jnp.float32)
+            )
+
+        for hop in range(count - 1):
+
+            @pl.when(jnp.logical_and(hop >= here, here < count - 1))
+            def _():
+                self.right(count - 1 + here - hop).wait_send()
+
+            @pl.when(jnp.logical_and(hop >= count - 1 - here, here > 0))
+            def _():
+                self.left(hop + here + 1 - count).wait_send()
+
+
+def gather_kernel(count, x_ref, out_ref, full, send_right, send_left, recv, done):
+    here = lax.axis_index("tensor")
+    rows = x_ref.shape[0]
+    line_barrier(here, count)
+    line = LineGather(here, count, rows, full, send_right, send_left, recv)
+    line.begin(x_ref)
+
+    def put(index):
+        return pltpu.make_async_copy(
+            block_of(full, index, rows), block_of(out_ref, index, rows), done.at[index]
+        )
+
+    own = pltpu.make_async_copy(x_ref, block_of(out_ref, here, rows), done.at[here])
+    own.start()
+    for hop in range(1, count):
+        line.arrive(hop, lambda index: put(index).start())
+    own.wait()
+    for index in range(count):
+
+        @pl.when(index != here)
+        def _():
+            put(index).wait()
+
+    line.finish()
+
+
+def line_gather(x, collective):
+    count = lax.axis_size("tensor")
+    rows, width = x.shape
+    return pl.pallas_call(
+        functools.partial(gather_kernel, count),
+        out_shape=jax.ShapeDtypeStruct((count * rows, width), x.dtype),
+        in_specs=[pl.BlockSpec(memory_space=pltpu.VMEM)],
+        out_specs=pl.BlockSpec(memory_space=pl.ANY),
+        scratch_shapes=[
+            pltpu.VMEM((count * rows, width), x.dtype),
+            pltpu.SemaphoreType.DMA((count,)),
+            pltpu.SemaphoreType.DMA((count,)),
+            pltpu.SemaphoreType.DMA((count,)),
+            pltpu.SemaphoreType.DMA((count,)),
+        ],
+        compiler_params=pltpu.CompilerParams(
+            collective_id=collective, has_side_effects=True, vmem_limit_bytes=VMEM_BYTES
+        ),
+        cost_estimate=pl.CostEstimate(
+            flops=0, transcendentals=0, bytes_accessed=64 * count * rows * width
+        ),
+    )(x)
+
+
+def scatter_kernel(
+    count, part_ref, out_ref, part, from_left, from_right, to_right, to_left, sems, got
+):
+    here = lax.axis_index("tensor")
+    rows = part.shape[1]
+    line_barrier(here, count)
+    line = LineScatter(here, count, from_left, from_right, to_right, to_left, sems)
+
+    def fetch(index):
+        return pltpu.make_async_copy(block_of(part_ref, index, rows), part.at[index], got.at[index])
+
+    for index in range(count):
+        fetch(index).start()
+    for index in range(count):
+        fetch(index).wait()
+    for hop in range(count - 1):
+        line.step(hop, lambda index: part[index])
+
+    def store(total):
+        out_ref[...] = total
+
+    line.finish(lambda: part[here].astype(jnp.float32), store)
+
+
+def line_scatter(parts, collective):
+    count = lax.axis_size("tensor")
+    rows, width = parts.shape[0] // count, parts.shape[1]
+    block = (count, rows, width)
+    return pl.pallas_call(
+        functools.partial(scatter_kernel, count),
+        out_shape=jax.ShapeDtypeStruct((rows, width), jnp.float32),
+        in_specs=[pl.BlockSpec(memory_space=pl.ANY)],
+        out_specs=pl.BlockSpec(memory_space=pltpu.VMEM),
+        scratch_shapes=[pltpu.VMEM(block, jnp.bfloat16)] * 5
+        + [pltpu.SemaphoreType.DMA((4, count)), pltpu.SemaphoreType.DMA((count,))],
+        compiler_params=pltpu.CompilerParams(
+            collective_id=collective, has_side_effects=True, vmem_limit_bytes=VMEM_BYTES
+        ),
+        cost_estimate=pl.CostEstimate(
+            flops=0, transcendentals=0, bytes_accessed=64 * count * rows * width
+        ),
+    )(parts)
+
+
+def total_kernel(line, planes, x_ref, out_ref, slots, send, recv):
+    plane, here = lax.axis_index("dp"), lax.axis_index("tensor")
+    me, everyone = plane * line + here, line * planes
+    barrier = pltpu.get_barrier_semaphore()
+
+    def greet(index, carry):
+        @pl.when(index != me)
+        def _():
+            pl.semaphore_signal(
+                barrier, inc=1, device_id=(index // line, index % line), device_id_type=MESH
+            )
+
+        return carry
+
+    lax.fori_loop(0, everyone, greet, 0)
+    pl.semaphore_wait(barrier, everyone - 1)
+
+    def to(index):
+        return pltpu.make_async_remote_copy(
+            src_ref=x_ref,
+            dst_ref=slots.at[me],
+            send_sem=send.at[index],
+            recv_sem=recv.at[me],
+            device_id=(index // line, index % line),
+            device_id_type=MESH,
+        )
+
+    def came(index):
+        return pltpu.make_async_remote_copy(
+            src_ref=x_ref,
+            dst_ref=slots.at[index],
+            send_sem=send.at[index],
+            recv_sem=recv.at[index],
+            device_id=(index // line, index % line),
+            device_id_type=MESH,
+        )
+
+    def push(index, carry):
+        @pl.when(index != me)
+        def _():
+            to(index).start()
+
+        return carry
+
+    lax.fori_loop(0, everyone, push, 0)
+    slots[me] = x_ref[...]
+
+    def settle(index, carry):
+        @pl.when(index != me)
+        def _():
+            came(index).wait_recv()
+            to(index).wait_send()
+
+        return carry
+
+    lax.fori_loop(0, everyone, settle, 0)
+
+    def add(index, total):
+        return total + slots[index]
+
+    out_ref[...] = lax.fori_loop(0, everyone, add, jnp.zeros(x_ref.shape, jnp.float32))
+
+
+def total_over_all(x, collective):
+    line, planes = lax.axis_size("tensor"), lax.axis_size("dp")
+    return pl.pallas_call(
+        functools.partial(total_kernel, line, planes),
+        out_shape=jax.ShapeDtypeStruct(x.shape, x.dtype),
+        in_specs=[pl.BlockSpec(memory_space=pltpu.VMEM)],
+        out_specs=pl.BlockSpec(memory_space=pltpu.VMEM),
+        scratch_shapes=[
+            pltpu.VMEM((line * planes,) + x.shape, x.dtype),
+            pltpu.SemaphoreType.DMA((line * planes,)),
+            pltpu.SemaphoreType.DMA((line * planes,)),
+        ],
+        compiler_params=pltpu.CompilerParams(collective_id=collective, has_side_effects=True),
+    )(x)
+
+
+def matmul(left, right, dims):
+    return lax.dot_general(left, right, (dims, ((), ())), preferred_element_type=jnp.float32)
+
+
+def over_sequences(function, operands):
+    if operands[0].shape[0] == 1:
+        results = function(tuple(operand[0] for operand in operands))
+        return tuple(result[None] for result in results)
+    return lax.map(function, operands)
+
+
 def per_device(
     hidden_in,
     query_proj,
@@ -130,22 +522,26 @@
     ffn_norm,
     cotangent,
 ):
-    query_full, key_full, value_full, gate_full, up_full = (
-        lax.all_gather(query_proj, "dp", axis=0, tiled=True),
-        lax.all_gather(key_proj, "dp", axis=0, tiled=True),
-        lax.all_gather(value_proj, "dp", axis=0, tiled=True),
-        lax.all_gather(gate_proj, "dp", axis=0, tiled=True),
-        lax.all_gather(up_proj, "dp", axis=0, tiled=True),
-    )
-    out_full, down_full = (
-        lax.all_gather(out_proj, "dp", axis=1, tiled=True),
-        lax.all_gather(down_proj, "dp", axis=1, tiled=True),
-    )
+    heads_width, kv_width, hidden_width = query_proj.shape[1], key_proj.shape[1], gate_proj.shape[1]
+    attn_full = lax.all_gather(
+        jnp.concatenate([query_proj, key_proj, value_proj, out_proj.T], axis=1),
+        "dp",
+        axis=0,
+        tiled=True,
+    )
+    gate_up_full = lax.all_gather(
+        jnp.concatenate([gate_proj, up_proj], axis=1), "dp", axis=0, tiled=True
+    )
+    down_full_t = lax.all_gather(down_proj.T, "dp", axis=0, tiled=True)
+    query_full, key_full, value_full, out_full_t = jnp.split(
+        attn_full, [heads_width, heads_width + kv_width, heads_width + 2 * kv_width], axis=1
+    )
+    gate_full, up_full = jnp.split(gate_up_full, 2, axis=1)
     local_rows = hidden_in.shape[0]
     score_scale = 1.0 / math.sqrt(HEAD_DIM)
     inputs = hidden_in.astype(jnp.float32)
     normed, unit_one, inv_one = norm_forward(inputs, attn_norm)
-    normed_bf = lax.all_gather(normed.astype(jnp.bfloat16), "tensor", axis=0, tiled=True)
+    normed_bf = line_gather(normed.astype(jnp.bfloat16), 0)
     group_rows = normed_bf.shape[0]
     local_heads = query_full.shape[1] // HEAD_DIM
     local_kv = key_full.shape[1] // HEAD_DIM
@@ -174,63 +570,45 @@
         jnp.bfloat16
     )
     key_rot = key_rot.reshape(sequences, SEQ_LEN, local_kv, HEAD_DIM)
-    attended, log_total = lax.map(
+    attended, log_total = over_sequences(
         lambda packed: attend_forward(packed[0], packed[1], packed[2], score_scale),
         (query_rot, key_rot, values_bf),
     )
     attended_flat = attended.reshape(group_rows, local_heads * HEAD_DIM)
-    rows_part = lax.slice_in_dim(attended_flat, 0, lax.axis_size("tensor") * local_rows, axis=0)
-    residual_mid = inputs + lax.psum_scatter(
-        jnp.dot(rows_part, out_full, preferred_element_type=jnp.float32).astype(jnp.bfloat16),
-        "tensor",
-        scatter_dimension=0,
-        tiled=True,
-    ).astype(jnp.float32)
+    residual_mid = inputs + line_scatter(
+        matmul(attended_flat, out_full_t, ((1,), (1,))).astype(jnp.bfloat16), 1
+    )
     ffn_normed, unit_two, inv_two = norm_forward(residual_mid, ffn_norm)
-    ffn_in = lax.all_gather(ffn_normed.astype(jnp.bfloat16), "tensor", axis=0, tiled=True)
+    ffn_in = line_gather(ffn_normed.astype(jnp.bfloat16), 2)
     gate_vals = jnp.dot(ffn_in, gate_full, preferred_element_type=jnp.float32)
     up_vals = jnp.dot(ffn_in, up_full, preferred_element_type=jnp.float32)
     sigmoid_gate = jax.nn.sigmoid(gate_vals)
     hidden_act = (gate_vals * sigmoid_gate * up_vals).astype(jnp.bfloat16)
-    rows_part = lax.slice_in_dim(hidden_act, 0, lax.axis_size("tensor") * local_rows, axis=0)
     hidden_out = (
         residual_mid
-        + lax.psum_scatter(
-            jnp.dot(rows_part, down_full, preferred_element_type=jnp.float32).astype(jnp.bfloat16),
-            "tensor",
-            scatter_dimension=0,
-            tiled=True,
-        ).astype(jnp.float32)
+        + line_scatter(matmul(hidden_act, down_full_t, ((1,), (1,))).astype(jnp.bfloat16), 3)
     ).astype(jnp.bfloat16)
-    cot_full = lax.all_gather(cotangent, "tensor", axis=0, tiled=True)
-    grad_hidden = jnp.dot(cot_full, down_full.T, preferred_element_type=jnp.float32)
-    down_grad = jnp.dot(hidden_act.T, cot_full, preferred_element_type=jnp.float32)
+    cot_full = line_gather(cotangent, 4)
+    grad_hidden = jnp.dot(cot_full, down_full_t, preferred_element_type=jnp.float32)
+    down_grad_t = matmul(cot_full, hidden_act, ((0,), (0,)))
     grad_up = (grad_hidden * (gate_vals * sigmoid_gate)).astype(jnp.bfloat16)
     grad_gate = (
         grad_hidden * up_vals * sigmoid_gate * (1.0 + gate_vals * (1.0 - sigmoid_gate))
     ).astype(jnp.bfloat16)
     gate_grad = jnp.dot(ffn_in.T, grad_gate, preferred_element_type=jnp.float32)
     up_grad = jnp.dot(ffn_in.T, grad_up, preferred_element_type=jnp.float32)
-    gate_part = lax.slice_in_dim(grad_gate, 0, lax.axis_size("tensor") * local_rows, axis=0)
-    up_part = lax.slice_in_dim(grad_up, 0, lax.axis_size("tensor") * local_rows, axis=0)
-    total = jnp.dot(gate_part, gate_full.T, preferred_element_type=jnp.float32)
-    grad_ffn_in = lax.psum_scatter(
-        (total + jnp.dot(up_part, up_full.T, preferred_element_type=jnp.float32)).astype(
-            jnp.bfloat16
-        ),
-        "tensor",
-        scatter_dimension=0,
-        tiled=True,
-    ).astype(jnp.float32)
+    total = jnp.dot(grad_gate, gate_full.T, preferred_element_type=jnp.float32)
+    total = total + jnp.dot(grad_up, up_full.T, preferred_element_type=jnp.float32)
+    grad_ffn_in = line_scatter(total.astype(jnp.bfloat16), 5)
     grad_part, ffn_gain_grad = norm_backward(grad_ffn_in, unit_two, inv_two, ffn_norm)
     grad_mid = cotangent.astype(jnp.float32) + grad_part
-    grad_mid_bf = lax.all_gather(grad_mid.astype(jnp.bfloat16), "tensor", axis=0, tiled=True)
-    out_grad = jnp.dot(attended_flat.T, grad_mid_bf, preferred_element_type=jnp.float32)
-    grad_attended = jnp.dot(grad_mid_bf, out_full.T, preferred_element_type=jnp.float32).astype(
+    grad_mid_bf = line_gather(grad_mid.astype(jnp.bfloat16), 6)
+    out_grad_t = matmul(grad_mid_bf, attended_flat, ((0,), (0,)))
+    grad_attended = jnp.dot(grad_mid_bf, out_full_t, preferred_element_type=jnp.float32).astype(
         jnp.bfloat16
     )
     grad_attended = grad_attended.reshape(sequences, SEQ_LEN, local_kv, groups, HEAD_DIM)
-    grad_query_rot, grad_key_rot, grad_vals = lax.map(
+    grad_query_rot, grad_key_rot, grad_vals = over_sequences(
         lambda packed: attend_backward(
             packed[0], packed[1], packed[2], packed[3], packed[4], packed[5], score_scale
         ),
@@ -250,45 +628,34 @@
     query_grad = jnp.dot(normed_bf.T, grad_queries_bf, preferred_element_type=jnp.float32)
     key_grad = jnp.dot(normed_bf.T, grad_keys_bf, preferred_element_type=jnp.float32)
     value_grad = jnp.dot(normed_bf.T, grad_vals_bf, preferred_element_type=jnp.float32)
-    value_part = lax.slice_in_dim(grad_vals_bf, 0, lax.axis_size("tensor") * local_rows, axis=0)
     total = jnp.dot(grad_queries_bf, query_full.T, preferred_element_type=jnp.float32)
     total = total + jnp.dot(grad_keys_bf, key_full.T, preferred_element_type=jnp.float32)
-    grad_normed_in = lax.psum_scatter(
-        (total + jnp.dot(value_part, value_full.T, preferred_element_type=jnp.float32)).astype(
-            jnp.bfloat16
-        ),
-        "tensor",
-        scatter_dimension=0,
-        tiled=True,
-    ).astype(jnp.float32)
+    total = total + jnp.dot(grad_vals_bf, value_full.T, preferred_element_type=jnp.float32)
+    grad_normed_in = line_scatter(total.astype(jnp.bfloat16), 7)
     grad_first, attn_gain_grad = norm_backward(grad_normed_in, unit_one, inv_one, attn_norm)
     dhidden_in = (grad_mid + grad_first).astype(jnp.bfloat16)
-    gain_totals = lax.psum(
-        (attn_gain_grad, query_gain_grad, key_gain_grad, ffn_gain_grad), ("dp", "tensor")
-    )
-    weight_sums = (
-        lax.psum_scatter(
-            query_grad.astype(jnp.bfloat16), "dp", scatter_dimension=0, tiled=True
-        ).astype(jnp.float32),
-        lax.psum_scatter(
-            key_grad.astype(jnp.bfloat16), "dp", scatter_dimension=0, tiled=True
-        ).astype(jnp.float32),
-        lax.psum_scatter(
-            value_grad.astype(jnp.bfloat16), "dp", scatter_dimension=0, tiled=True
-        ).astype(jnp.float32),
-        lax.psum_scatter(
-            out_grad.astype(jnp.bfloat16), "dp", scatter_dimension=1, tiled=True
-        ).astype(jnp.float32),
-        lax.psum_scatter(
-            gate_grad.astype(jnp.bfloat16), "dp", scatter_dimension=0, tiled=True
-        ).astype(jnp.float32),
-        lax.psum_scatter(
-            up_grad.astype(jnp.bfloat16), "dp", scatter_dimension=0, tiled=True
-        ).astype(jnp.float32),
-        lax.psum_scatter(
-            down_grad.astype(jnp.bfloat16), "dp", scatter_dimension=1, tiled=True
-        ).astype(jnp.float32),
-    )
+    gains = (attn_gain_grad, query_gain_grad, key_gain_grad, ffn_gain_grad)
+    lengths = [gain.shape[0] for gain in gains]
+    packed = jnp.concatenate(gains)
+    gain_total = total_over_all(packed.reshape(-1, HEAD_DIM), 8).reshape(-1)
+    gain_totals = jnp.split(gain_total, [sum(lengths[:k]) for k in range(1, len(lengths))])
+
+    def scatter(parts):
+        return lax.psum_scatter(
+            jnp.concatenate([part.astype(jnp.bfloat16) for part in parts], axis=1),
+            "dp",
+            scatter_dimension=0,
+            tiled=True,
+        ).astype(jnp.float32)
+
+    down_sum_t = scatter([down_grad_t])
+    gate_sum, up_sum = jnp.split(scatter([gate_grad, up_grad]), 2, axis=1)
+    query_sum, key_sum, value_sum, out_sum_t = jnp.split(
+        scatter([query_grad, key_grad, value_grad, out_grad_t]),
+        [heads_width, heads_width + kv_width, heads_width + 2 * kv_width],
+        axis=1,
+    )
+    weight_sums = (query_sum, key_sum, value_sum, out_sum_t.T, gate_sum, up_sum, down_sum_t.T)
     return (
         hidden_out,
         dhidden_in,

time: 1330 us -> 895 us (0.67)
  waiting for transfers between devices: 996 us -> 0.81 us
  Pallas kernels: 0 us -> 587 us
  blocking collectives: 46.3 us -> 0 us
  other arithmetic: 53.7 us -> 69.8 us
  matrix products: 191 us -> 175 us
  local copies, waits for them, and re-layouts: 15.7 us -> 30.7 us
    pallas_call x0 -> x9, Pallas kernels: none -> 587 us  [the longest x4 291 us: line_scatter(): pl.pallas_call(functools.partial(scatter_kernel, count), out_shape=jax.Sh...]
    reduce_scatter x11 -> x3, waiting for transfers between devices: 523 us -> 0.01 us  [scatter(): lax.psum_scatter(jnp.concatenate([part.astype(jnp.bfloat16) for part in p...]
    all_gather x11 -> x3, waiting for transfers between devices: 468 us -> 0.02 us  [the longest x1 0.02 us: per_device(): down_full_t = lax.all_gather(down_proj.T, 'dp', axis=0, tiled=True)]
    psum x1 -> x0, blocking collectives: 46.3 us -> none  [per_device(): lax.psum((attn_gain_grad, query_gain_grad, key_gain_grad, ffn_gain_grad),...]
    concatenate x0 -> x4, other arithmetic: none -> 31.1 us  [the longest x2 27.8 us: scatter(): jnp.concatenate([part.astype(jnp.bfloat16) for part in parts], axis=1)]
    convert_element_type x10 -> x4, other arithmetic: 22.5 us -> 4.24 us  [the longest x1 1.63 us: per_device(): grad_mid_bf = line_gather(grad_mid.astype(jnp.bfloat16), 6)]
  transfers between devices with their start and end apart: 22 -> 6, of which waited for: 21 -> 0; matrix products, arithmetic and copies ran while one was open for 15% -> 16% of each run, Pallas kernels for 0% -> 51%
where the time goes in v1:
time: 895 us; the launch traced here: 879 us
  Pallas kernels  587 us (66%)
  matrix products  175 us (20%)
  other arithmetic  69.8 us (8%)
  local copies, waits for them, and re-layouts  30.7 us (3%)
  between operations  15.6 us (2%)
    pallas_call x4, Pallas kernels, line_scatter(): pl.pallas_call(functools.partial(scatter_kernel, count), out_shape=jax.Sh...  291 us
    pallas_call x4, Pallas kernels, line_gather(): pl.pallas_call(functools.partial(gather_kernel, count), out_shape=jax.Sha...  274 us
    dot_general x4, matrix products, matmul(): lax.dot_general(left, right, (dims, ((), ())), preferred_element_type=jnp...  30.9 us
    concatenate x2, other arithmetic, scatter(): jnp.concatenate([part.astype(jnp.bfloat16) for part in parts], axis=1)  27.8 us
    unnamed x162, local copies, waits for them, and re-layouts  22.6 us
    pallas_call x1, Pallas kernels, total_over_all(): pl.pallas_call(functools.partial(total_kernel, line, planes), out_shape=j...  22.2 us
  transfers between devices with their start and end apart: 6, of which 0 were waited for; matrix products, arithmetic and copies ran while one was open for 16% of the time, Pallas kernels for 51%

profile of v1, /device:TPU:9, one launch (start us, length us, event | category | flops | bytes accessed | tf_op | source)
XLA Modules:
  0.0 879.4 jit_solution(1363281309422122165)
XLA Ops:
  16.3 70.1 %shard_map.228 = bf16[1024,2048]{1,0:T(8,128)(2,1)} custom-call(bf16[256,2048]{1,0:T(8,128)(2,1)} %fusion.26.x_ref), custom_call_target="tpu_custom_call" | custom-call | bytes 134217728 | tf_op jit(solution)/shard_map/pallas_call | solution.py:355
  86.5 70.3 %shard_map.232 = bf16[1024,2048]{1,0:T(8,128)(2,1)} custom-call(bf16[256,2048]{1,0:T(8,128)(2,1)} %x_ref.1), custom_call_target="tpu_custom_call" | custom-call | bytes 134217728 | tf_op jit(solution)/shard_map/pallas_call | solution.py:355
  162.3 5.3 multiply_reduce_fusion.4
  199.5 73.3 %shard_map.229 = f32[256,2048]{1,0:T(8,128)} custom-call(bf16[1024,2048]{1,0:T(8,128)(2,1)} %convolution_convert_fusion.4.part_ref), custom_call_target="tpu_custom_call" | custom-call | bytes 134217728 | tf_op jit(solution)/shard_map/pallas_call | solution.py:404
  276.3 67.1 %shard_map.230 = bf16[1024,2048]{1,0:T(8,128)(2,1)} custom-call(bf16[256,2048]{1,0:T(8,128)(2,1)} %multiply_convert_fusion.3.x_ref), custom_call_target="tpu_custom_call" | custom-call | bytes 134217728 | tf_op jit(solution)/shard_map/pallas_call | solution.py:355
  343.5 11.7 %fusion.85 = f32[1024,1536]{1,0:T(8,128)} fusion(bf16[1024,2048]{1,0:T(8,128)(2,1)} %shard_map.232, bf16[2048,1536]{0,1:T(8,128)(2,1)} %all-gather.8.cloned.1.call-done), kind=kOutput, calls=%fused_computation.175 | convolution fusion | flops 6442450944 | bytes 16777216 | tf_op jit(solution)/shard_map/dot_general | solution.py:592
  355.2 11.9 %fusion.12 = f32[1024,1536]{1,0:T(8,128)} fusion(bf16[1024,2048]{1,0:T(8,128)(2,1)} %shard_map.230, bf16[2048,3072]{1,0:T(8,128)(2,1)} %all-gather.6.cloned.1.call-done), kind=kOutput, calls=%fused_computation.31 | convolution fusion | flops 6442450944 | bytes 16777216 | tf_op jit(solution)/shard_map/dot_general | solution.py:584
  367.1 15.4 %multiply_convert_fusion.1 = (bf16[1024,1536]{1,0:T(8,128)(2,1)}, bf16[1024,1536]{1,0:T(8,128)(2,1)}, bf16[1024,1536]{1,0:T(8,128)(2,1)}) fusion(f32[1024,1536]{1,0:T(8,128)S(1)} %copy-done.68, f32[1024,1536]{1,0:T(8,128)} %fusion.12, bf16[1024,2048]{1,0:T(8,128)(2,1)S(1)} %copy-done.35, bf16[2048,3072]{1,0:T(8,128)(2,1)} %all-gather.6.cloned.1.call-done), kind=kOutput, calls=%fused_computation.25 | convolution fusion | flops 6466043904 | bytes 32505856 | tf_op jit(solution)/shard_map/dot_general | solution.py:583
  382.5 12.1 %fusion.10 = f32[1024,2048]{1,0:T(8,128)} fusion(bf16[1024,1536]{1,0:T(8,128)(2,1)} %get-tuple-element.51, bf16[2048,3072]{1,0:T(8,128)(2,1)} %all-gather.6.cloned.1.call-done), kind=kOutput, calls=%fused_computation.29 | convolution fusion | flops 6442450944 | bytes 17825792 | tf_op jit(solution)/shard_map/dot_general | solution.py:601
  394.6 10.8 %add_convert_fusion.1.part_ref = bf16[1024,2048]{1,0:T(8,128)(2,1)} fusion(f32[1024,2048]{1,0:T(8,128)} %fusion.10, bf16[1024,1536]{1,0:T(8,128)(2,1)S(1)} %copy-done.69, bf16[2048,3072]{1,0:T(8,128)(2,1)S(1)} %copy-done.65), kind=kOutput, calls=%fused_computation.12 | convolution fusion | flops 6446645248 | bytes 22020096 | tf_op jit(solution)/shard_map/dot_general | solution.py:600
  405.4 72.2 %shard_map.233 = f32[256,2048]{1,0:T(8,128)} custom-call(bf16[1024,2048]{1,0:T(8,128)(2,1)} %add_convert_fusion.1.part_ref), custom_call_target="tpu_custom_call" | custom-call | bytes 134217728 | tf_op jit(solution)/shard_map/pallas_call | solution.py:404
  481.7 66.5 %shard_map.234 = bf16[1024,2048]{1,0:T(8,128)(2,1)} custom-call(bf16[256,2048]{1,0:T(8,128)(2,1)} %fusion.78.x_ref), custom_call_target="tpu_custom_call" | custom-call | bytes 134217728 | tf_op jit(solution)/shard_map/pallas_call | solution.py:355
  548.3 5.3 fusion.50
  554.1 6.0 convolution_bitcast_fusion
  598.2 12.4 %pad_maximum_fusion.1 = bf16[2048,1536]{0,1:T(8,128)(2,1)} fusion(bf16[2048,512]{0,1:T(8,128)(2,1)S(1)} %copy-done.41, bf16[2048,256]{0,1:T(8,128)(2,1)S(1)} %convolution_convert_fusion.7, bf16[2048,256]{0,1:T(8,128)(2,1)S(1)} %convolution_convert_fusion.8, bf16[2048,512]{0,1:T(8,128)(2,1)S(1)} %convolution_convert_fusion.6), kind=kLoop, calls=%fused_computation.23 | loop fusion | flops 25165824 | bytes 12582912 | tf_op jit(solution)/shard_map/concatenate | solution.py:645
  610.7 11.3 %fusion.8 = bf16[2048,1536]{0,1:T(8,128)(2,1)} fusion(bf16[1024,1536]{1,0:T(8,128)(2,1)} %get-tuple-element.52, bf16[1024,2048]{1,0:T(8,128)(2,1)} %shard_map.232), kind=kOutput, calls=%fused_computation.22 | convolution fusion | flops 6445596672 | bytes 13631488 | tf_op jit(solution)/shard_map/dot_general | solution.py:500
  622.1 10.7 %convolution_convert_fusion.1 = bf16[2048,1536]{0,1:T(8,128)(2,1)S(1)} fusion(bf16[1024,2048]{1,0:T(8,128)(2,1)} %shard_map.230, bf16[1024,1536]{1,0:T(8,128)(2,1)} %get-tuple-element.51), kind=kOutput, calls=%fused_computation.18 | convolution fusion | flops 6445596672 | bytes 13631488 | tf_op jit(solution)/shard_map/dot_general | solution.py:599
  632.8 7.5 convolution_convert_fusion.2
  640.3 15.4 %pad_maximum_fusion = bf16[2048,3072]{0,1:T(8,128)(2,1)} fusion(bf16[2048,1536]{0,1:T(8,128)(2,1)S(1)} %convolution_convert_fusion.1, bf16[2048,1536]{0,1:T(8,128)(2,1)S(1)} %convolution_convert_fusion.2), kind=kLoop, calls=%fused_computation | loop fusion | flops 25165824 | bytes 25165824 | tf_op jit(solution)/shard_map/concatenate | solution.py:645
  668.2 72.4 %shard_map.235 = f32[256,2048]{1,0:T(8,128)} custom-call(bf16[1024,2048]{1,0:T(8,128)(2,1)} %add_convert_fusion.part_ref), custom_call_target="tpu_custom_call" | custom-call | bytes 134217728 | tf_op jit(solution)/shard_map/pallas_call | solution.py:404
  743.6 22.2 %shard_map.236 = f32[34,128]{1,0:T(8,128)} custom-call(f32[34,128]{1,0:T(8,128)} %maximum_bitcast_fusion.x_ref), custom_call_target="tpu_custom_call" | custom-call | tf_op jit(solution)/shard_map/pallas_call | solution.py:485
  765.8 11.5 %convolution_convert_fusion.3.part_ref = bf16[1024,2048]{1,0:T(8,128)(2,1)} fusion(bf16[1024,1536]{1,0:T(8,128)(2,1)} %get-tuple-element.52, bf16[2048,1536]{0,1:T(8,128)(2,1)} %all-gather.8.cloned.1.call-done), kind=kOutput, calls=%fused_computation.39 | convolution fusion | flops 6444548096 | bytes 13631488 | tf_op jit(solution)/shard_map/dot_general | solution.py:500
  777.3 72.9 %shard_map.231 = f32[256,2048]{1,0:T(8,128)} custom-call(bf16[1024,2048]{1,0:T(8,128)(2,1)} %convolution_convert_fusion.3.part_ref), custom_call_target="tpu_custom_call" | custom-call | bytes 134217728 | tf_op jit(solution)/shard_map/pallas_call | solution.py:404
  851.3 5.6 fusion.31
  (264 shorter events, 123.8 us)
Async XLA Ops:
  7.2 155.1 %all-gather.4.cloned.1.call-start = ((), (), s32[]{:S(2)}) async-start(), calls=%async_computation.3 | async-start | bytes 7077888 | tf_op jit(solution)/shard_map/all_gather | solution.py:526
  8.4 6.3 copy-start.6
  12.5 331.0 %all-gather.8.cloned.1.call-start = ((), (), s32[]{:S(2)}) async-start(), calls=%async_computation.5 | async-start | bytes 7077888 | tf_op jit(solution)/shard_map/all_gather | solution.py:535
  13.2 341.9 %all-gather.6.cloned.1.call-start = ((), (), s32[]{:S(2)}) async-start(), calls=%async_computation.4 | async-start | bytes 14155776 | tf_op jit(solution)/shard_map/all_gather | solution.py:532
  14.7 842.2 %reduce-scatter.4.cloned.1.call-start = ((), (), s32[]{:S(2)}) async-start(), calls=%async_computation.6 | async-start | bytes 7077888 | tf_op jit(solution)/shard_map/reduce_scatter | solution.py:644
  15.0 141.7 %copy-start.60 = (f32[256]{0:T(256)}, f32[256]{0:T(256)S(1)}, u32[]{:S(2)}) copy-start(f32[256]{0:T(256)S(1)} %add_rsqrt_fusion.3) | copy-start | bytes 3076
  86.4 74.1 %copy-start.62 = (f32[128]{0:T(128)S(1)}, f32[128]{0:T(128)}, u32[]{:S(2)}) copy-start(f32[128]{0:T(128)} %param.22) | copy-start | bytes 1540
  177.4 11.6 %copy-start.4 = (f32[2,1024,512,2]{2,1,3,0:T(8,128)}, f32[2,1024,512,2]{2,1,3,0:T(8,128)S(1)}, u32[]{:S(2)}) copy-start(f32[2,1024,512,2]{2,1,3,0:T(8,128)S(1)} %get-tuple-element.88) | copy-start | bytes 25165828
  181.1 10.4 %copy-start.3 = (f32[2,1024,512,2]{2,1,3,0:T(8,128)}, f32[2,1024,512,2]{2,1,3,0:T(8,128)S(1)}, u32[]{:S(2)}) copy-start(f32[2,1024,512,2]{2,1,3,0:T(8,128)S(1)} %get-tuple-element.86) | copy-start | bytes 25165828
  181.1 6.6 copy-start.33
  355.2 11.9 %copy-start.35 = (bf16[1024,2048]{1,0:T(8,128)(2,1)S(1)}, bf16[1024,2048]{1,0:T(8,128)(2,1)}, u32[]{:S(2)}) copy-start(bf16[1024,2048]{1,0:T(8,128)(2,1)} %shard_map.230) | copy-start | bytes 12582916
  355.2 11.9 %copy-start.68 = (f32[1024,1536]{1,0:T(8,128)S(1)}, f32[1024,1536]{1,0:T(8,128)}, u32[]{:S(2)}) copy-start(f32[1024,1536]{1,0:T(8,128)} %fusion.85) | copy-start | bytes 18874372
  382.5 12.1 %copy-start.65 = (bf16[2048,3072]{1,0:T(8,128)(2,1)S(1)}, bf16[2048,3072]{1,0:T(8,128)(2,1)}, u32[]{:S(2)}) copy-start(bf16[2048,3072]{1,0:T(8,128)(2,1)} %all-gather.6.cloned.1.call-done) | copy-start | bytes 37748740
  382.5 12.1 %copy-start.69 = (bf16[1024,1536]{1,0:T(8,128)(2,1)S(1)}, bf16[1024,1536]{1,0:T(8,128)(2,1)}, u32[]{:S(2)}) copy-start(bf16[1024,1536]{1,0:T(8,128)(2,1)} %get-tuple-element.50) | copy-start | bytes 9437188
  553.6 6.5 slice-start.2
  566.9 17.9 %copy-start.15 = (f32[2,128,2,512]{3,1,2,0:T(8,128)}, f32[2,128,2,512]{3,1,2,0:T(8,128)S(1)}, u32[]{:S(2)}) copy-start(f32[2,128,2,512]{3,1,2,0:T(8,128)S(1)} %fusion.87) | copy-start | bytes 3145732
  610.6 252.0 %reduce-scatter.8.cloned.1.call-start = ((), (), s32[]{:S(2)}) async-start(), calls=%async_computation.8 | async-start | bytes 7077888 | tf_op jit(solution)/shard_map/reduce_scatter | solution.py:644
  622.0 243.0 %reduce-scatter.6.cloned.1.call-start = ((), (), s32[]{:S(2)}) async-start(), calls=%async_computation.7 | async-start | bytes 14155776 | tf_op jit(solution)/shard_map/reduce_scatter | solution.py:644
  622.0 10.7 %copy-start.36 = (bf16[1024,2048]{1,0:T(8,128)(2,1)S(1)}, bf16[1024,2048]{1,0:T(8,128)(2,1)}, u32[]{:S(2)}) copy-start(bf16[1024,2048]{1,0:T(8,128)(2,1)} %shard_map.230) | copy-start | bytes 12582916
  622.1 10.7 %copy-start.70 = (bf16[1024,1536]{1,0:T(8,128)(2,1)S(1)}, bf16[1024,1536]{1,0:T(8,128)(2,1)}, u32[]{:S(2)}) copy-start(bf16[1024,1536]{1,0:T(8,128)(2,1)} %get-tuple-element.50) | copy-start | bytes 9437188
  668.2 72.4 %copy-start.7 = (bf16[256,2048]{1,0:T(8,128)(2,1)S(1)}, bf16[256,2048]{1,0:T(8,128)(2,1)}, u32[]{:S(2)}) copy-start(bf16[256,2048]{1,0:T(8,128)(2,1)} %param.13) | copy-start | bytes 3145732
  668.2 72.4 %copy-start.58 = (f32[2048]{0:T(1024)S(1)}, f32[2048]{0:T(1024)}, u32[]{:S(2)}) copy-start(f32[2048]{0:T(1024)} %param.21) | copy-start | bytes 24580
  668.2 72.4 %copy-start.61 = (f32[256]{0:T(256)S(1)}, f32[256]{0:T(256)}, u32[]{:S(2)}) copy-start(f32[256]{0:T(256)} %copy-done.60) | copy-start | bytes 3076
  777.3 72.9 %copy-start.59 = (f32[34,128]{1,0:T(8,128)S(1)}, f32[34,128]{1,0:T(8,128)}, u32[]{:S(2)}) copy-start(f32[34,128]{1,0:T(8,128)} %shard_map.236) | copy-start | bytes 52228
  (59 other events, 206.0 us)
Sparse Core Ops, SparseCore 0:
  12.6 48.1 all-gather.3
  62.7 46.5 all-gather.7
  111.7 71.9 all-gather.5
  610.7 68.0 reduce-scatter.3
  682.1 61.5 reduce-scatter.7
  747.1 91.9 reduce-scatter.5

commit v2 on v1

v2 whole, which is shorter than its diff:
```python
import functools
import math

import jax
import jax.numpy as jnp
from jax import lax
from jax.experimental import pallas as pl
from jax.experimental.pallas import tpu as pltpu
from jax.sharding import PartitionSpec as P

HEAD_DIM = 128
SEQ_LEN = 1024


EPSILON = 1e-06
ROPE_BASE = 1000000.0
NEG_FILL = -1e30
MESH = pl.DeviceIdType.MESH
VMEM_BYTES = 63 * 2**20
TILE = 512
F32, BF16 = jnp.float32, jnp.bfloat16
NN, NT, TN = ((1,), (0,)), ((1,), (1,)), ((0,), (0,))
IN_VMEM, IN_HBM = pl.BlockSpec(memory_space=pltpu.VMEM), pl.BlockSpec(memory_space=pl.ANY)
DMA = pltpu.SemaphoreType.DMA


def matmul(left, right, dims):
    return lax.dot_general(left, right, (dims, ((), ())), preferred_element_type=F32)


def tile_of(size):
    return TILE if size % TILE == 0 else size


def span(index, size):
    return pl.ds(pl.multiple_of(index * size, size), size)


def loop(start, stop, body):
    lax.fori_loop(start, stop, lambda index, carry: (body(index), carry)[1], 0)


def params(collective=None):
    return pltpu.CompilerParams(
        collective_id=collective, has_side_effects=True, vmem_limit_bytes=VMEM_BYTES
    )


def greet_line(here, count):
    barrier = pltpu.get_barrier_semaphore()

    @pl.when(here > 0)
    def _():
        pl.semaphore_signal(barrier, inc=1, device_id={"tensor": here - 1}, device_id_type=MESH)

    @pl.when(here < count - 1)
    def _():
        pl.semaphore_signal(barrier, inc=1, device_id={"tensor": here + 1}, device_id_type=MESH)


def meet_line(here, count):
    barrier = pltpu.get_barrier_semaphore()
    inside = jnp.logical_and(here > 0, here < count - 1)

    @pl.when(inside)
    def _():
        pl.semaphore_wait(barrier, 2)

    @pl.when(jnp.logical_not(inside))
    def _():
        pl.semaphore_wait(barrier, 1)


class LineGather:
    def __init__(self, here, count, rows, full, sems):
        self.here, self.count, self.rows, self.full, self.sems = here, count, rows, full, sems

    def copy(self, index, step, src=None):
        block = self.full.at[span(index, self.rows)]
        return pltpu.make_async_remote_copy(
            src_ref=block if src is None else src,
            dst_ref=block,
            send_sem=self.sems.at[0 if step > 0 else 1, index],
            recv_sem=self.sems.at[2, index],
            device_id={"tensor": self.here + step},
            device_id_type=MESH,
        )

    def begin(self, own=None):
        @pl.when(self.here < self.count - 1)
        def _():
            self.copy(self.here, 1, own).start()

        @pl.when(self.here > 0)
        def _():
            self.copy(self.here, -1, own).start()

    def arrive(self, hop):
        here, count = self.here, self.count

        @pl.when(here >= hop)
        def _():
            self.copy(here - hop, 1).wait_recv()

            @pl.when(here < count - 1)
            def _():
                self.copy(here - hop, 1).start()

        @pl.when(here < count - hop)
        def _():
            self.copy(here + hop, -1).wait_recv()

            @pl.when(here > 0)
            def _():
                self.copy(here + hop, -1).start()

    def each(self, hop, then):
        def side(which):
            index = self.here + (2 * which - 1) * hop
            fits = jnp.logical_and(index >= 0, index < self.count)

            @pl.when(jnp.logical_and(fits, which + hop > 0))
            def _():
                then(index)

        loop(0, 2, side)

    def finish(self):
        here, count = self.here, self.count

        def settle(hop):
            @pl.when(jnp.logical_and(here >= hop, here < count - 1))
            def _():
                self.copy(here - hop, 1).wait_send()

            @pl.when(jnp.logical_and(here < count - hop, here > 0))
            def _():
                self.copy(here + hop, -1).wait_send()

        loop(0, count, settle)


class LineScatter:
    def __init__(self, here, count, came, going, sems):
        self.here, self.count, self.came, self.going, self.sems = here, count, came, going, sems

    def right(self, index):
        return pltpu.make_async_remote_copy(
            src_ref=self.going.at[index],
            dst_ref=self.came.at[index + 1],
            send_sem=self.sems.at[0, index],
            recv_sem=self.sems.at[1, index],
            device_id={"tensor": self.here + 1},
            device_id_type=MESH,
        )

    def left(self, index):
        return pltpu.make_async_remote_copy(
            src_ref=self.going.at[index],
            dst_ref=self.came.at[index],
            send_sem=self.sems.at[2, index],
            recv_sem=self.sems.at[3, index],
            device_id={"tensor": self.here - 1},
            device_id_type=MESH,
        )

    def goes_right(self, hop):
        return jnp.logical_and(hop >= self.here, self.here < self.count - 1)

    def goes_left(self, hop):
        return jnp.logical_and(hop >= self.count - 1 - self.here, self.here > 0)

    def rightward(self, hop):
        return self.count - 1 + self.here - hop

    def leftward(self, hop):
        return hop + self.here + 1 - self.count

    def each(self, hop, then):
        def side(which):
            goes = jnp.where(which == 0, self.goes_right(hop), self.goes_left(hop))

            @pl.when(goes)
            def _():
                then((1 - which) * self.rightward(hop) + which * self.leftward(hop))

        loop(0, 2, side)

    def add(self, index, slot):
        self.going[index] = (
            self.going[index].astype(F32) + self.came[slot].astype(F32)
        ).astype(BF16)

    def step(self, hop):
        here, count = self.here, self.count

        @pl.when(self.goes_right(hop))
        def _():
            index = self.rightward(hop)

            @pl.when(here > 0)
            def _():
                self.right(index).wait_recv()
                self.add(index, index + 1)

            self.right(index).start()

        @pl.when(self.goes_left(hop))
        def _():
            index = self.leftward(hop)

            @pl.when(here < count - 1)
            def _():
                self.left(index).wait_recv()
                self.add(index, index)

            self.left(index).start()

    def finish(self, total):
        here, count = self.here, self.count

        @pl.when(here > 0)
        def _():
            self.right(here).wait_recv()
            total[...] += self.came[here + 1].astype(F32)

        @pl.when(here < count - 1)
        def _():
            self.left(here).wait_recv()
            total[...] += self.came[here].astype(F32)

        def settle(hop):
            @pl.when(self.goes_right(hop))
            def _():
                self.right(self.rightward(hop)).wait_send()

            @pl.when(self.goes_left(hop))
            def _():
                self.left(self.leftward(hop)).wait_send()

        loop(0, count - 1, settle)


def scatter_scratch(count, rows, width):
    return [
        pltpu.VMEM((count + 1, rows, width), BF16),
        pltpu.VMEM((count, rows, width), BF16),
        DMA((4, count)),
    ]


def gather_scratch(count, rows, width):
    return [pltpu.VMEM((count * rows, width), BF16), DMA((3, count))]


def row_blocks(rows):
    return 64 if rows % 64 == 0 else rows


def norm_rows(values_ref, gain_ref, store):
    block = row_blocks(values_ref.shape[0])

    def body(index):
        rows = span(index, block)
        values = values_ref[rows, :].astype(F32)
        inverse = lax.rsqrt(jnp.mean(values * values, axis=-1, keepdims=True) + EPSILON)
        store(rows, values * inverse * gain_ref[...])

    loop(0, values_ref.shape[0] // block, body)


def norm_rows_backward(grad_ref, values_ref, gain_ref, gain_grad_ref, store):
    block = row_blocks(values_ref.shape[0])
    gain_grad_ref[...] = jnp.zeros_like(gain_grad_ref)

    def body(index):
        rows = span(index, block)
        values, grad = values_ref[rows, :].astype(F32), grad_ref[rows, :]
        inverse = lax.rsqrt(jnp.mean(values * values, axis=-1, keepdims=True) + EPSILON)
        unit = values * inverse
        grad_unit = grad * gain_ref[...]
        mean = jnp.mean(grad_unit * unit, axis=-1, keepdims=True)
        gain_grad_ref[...] += jnp.sum(grad * unit, axis=0, keepdims=True)
        store(rows, inverse * (grad_unit - unit * mean))

    loop(0, values_ref.shape[0] // block, body)


def first_kernel(count, hidden_ref, gain_ref, out_ref, full, sems, done):
    here = lax.axis_index("tensor")
    rows = hidden_ref.shape[0]
    greet_line(here, count)
    own = full.at[span(here, rows)]

    def store(block, normed):
        own[block, :] = normed.astype(BF16)

    norm_rows(hidden_ref, gain_ref, store)
    meet_line(here, count)
    line = LineGather(here, count, rows, full, sems)
    line.begin()

    def put(index):
        return pltpu.make_async_copy(
            full.at[span(index, rows)], out_ref.at[span(index, rows)], done.at[index]
        )

    def pass_on(hop):
        @pl.when(hop > 0)
        def _():
            line.arrive(hop)

        line.each(hop, lambda index: put(index).start())

    loop(0, count, pass_on)
    loop(0, count, lambda index: put(index).wait())
    line.finish()


def first_gather(hidden, gain, collective):
    count = lax.axis_size("tensor")
    rows, width = hidden.shape
    return pl.pallas_call(
        functools.partial(first_kernel, count),
        out_shape=jax.ShapeDtypeStruct((count * rows, width), BF16),
        in_specs=[IN_VMEM, IN_VMEM],
        out_specs=IN_HBM,
        scratch_shapes=gather_scratch(count, rows, width) + [DMA((count,))],
        compiler_params=params(collective),
        cost_estimate=pl.CostEstimate(
            flops=0, transcendentals=0, bytes_accessed=64 * count * rows * width
        ),
        name="first_gather",
    )(hidden, gain[None])


def middle_kernel(
    count, attended, weights, hidden_ref, cot_ref, mid_ref, cot_out,
    came, going, scatter_sems, full, gather_sems, done,
):
    here = lax.axis_index("tensor")
    rows, width = hidden_ref.shape
    tile = tile_of(width)
    out_columns = slice(weights.shape[1] - attended.shape[1], weights.shape[1])
    greet_line(here, count)

    def term(index, store):
        left = attended[span(index, rows), :]

        def column(k):
            store(span(k, tile), matmul(left, weights[span(k, tile), out_columns], NT))

        loop(0, width // tile, column)

    def part(index):
        def store(columns, value):
            going[index, :, columns] = value.astype(BF16)

        term(index, store)

    scatter = LineScatter(here, count, came, going, scatter_sems)
    gather = LineGather(here, count, rows, full, gather_sems)

    def put(index):
        return pltpu.make_async_copy(
            full.at[span(index, rows)], cot_out.at[span(index, rows)], done.at[index]
        )

    own = pltpu.make_async_copy(cot_ref, cot_out.at[span(here, rows)], done.at[here])
    own.start()
    scatter.each(0, part)
    meet_line(here, count)
    scatter.step(0)
    gather.begin(cot_ref)

    def own_term(columns, value):
        mid_ref[:, columns] = hidden_ref[:, columns].astype(F32) + value

    term(here, own_term)

    def pass_on(hop):
        scatter.each(hop, part)
        scatter.step(hop)
        gather.arrive(hop)
        gather.each(hop, lambda index: put(index).start())

    loop(1, count - 1, pass_on)
    gather.arrive(count - 1)
    gather.each(count - 1, lambda index: put(index).start())
    scatter.finish(mid_ref)
    own.wait()

    def settle(index):
        @pl.when(index != here)
        def _():
            put(index).wait()

    loop(0, count, settle)
    gather.finish()


def middle_scatter(attended, weights, hidden, cotangent, collective):
    count = lax.axis_size("tensor")
    rows, width = hidden.shape
    return pl.pallas_call(
        functools.partial(middle_kernel, count),
        out_shape=[
            jax.ShapeDtypeStruct((rows, width), F32),
            jax.ShapeDtypeStruct((count * rows, width), BF16),
        ],
        in_specs=[IN_VMEM] * 4,
        out_specs=[IN_VMEM, IN_HBM],
        scratch_shapes=scatter_scratch(count, rows, width)
        + gather_scratch(count, rows, width)
        + [DMA((count,))],
        compiler_params=params(collective),
        cost_estimate=pl.CostEstimate(
            flops=0, transcendentals=0, bytes_accessed=80 * count * rows * width
        ),
        name="middle_scatter",
    )(attended, weights, hidden, cotangent)


def ffn_kernel(
    count, mid_ref, gain_ref, cot_hbm, gate_up_hbm, down_hbm,
    grad_mid, gain_grad, out_part, weight_grad,
    full, gather_sems, came, going, scatter_sems,
    cot, gate_up, down_t, act, grads, stage, loads, stores,
):
    here = lax.axis_index("tensor")
    rows, width = mid_ref.shape
    hidden = down_t.shape[1]
    cols, tile = tile_of(hidden), tile_of(width)
    greet_line(here, count)
    fetches = [
        pltpu.make_async_copy(src, dst, loads.at[k])
        for k, (src, dst) in enumerate(
            ((cot_hbm, cot), (down_hbm, down_t), (gate_up_hbm, gate_up))
        )
    ]
    for fetch in fetches:
        fetch.start()
    own = full.at[span(here, rows)]

    def store_normed(block, normed):
        own[block, :] = normed.astype(BF16)

    norm_rows(mid_ref, gain_ref, store_normed)
    meet_line(here, count)
    gather = LineGather(here, count, rows, full, gather_sems)
    scatter = LineScatter(here, count, came, going, scatter_sems)
    gather.begin()
    fetches[0].wait()
    fetches[1].wait()

    def grad_hidden(index):
        block, columns = span(index // (hidden // cols), rows), span(index % (hidden // cols), cols)
        grads[block, columns] = matmul(cot[block, :], down_t[:, columns], NN).astype(BF16)

    loop(0, count * (hidden // cols), grad_hidden)
    fetches[2].wait()

    def forward(index):
        block = span(index, rows)

        def column(k):
            here_cols, up_cols = span(k, cols), pl.ds(pl.multiple_of(hidden + k * cols, cols), cols)
            gate = matmul(full[block, :], gate_up[:, here_cols], NN)
            up = matmul(full[block, :], gate_up[:, up_cols], NN)
            grad = grads[block, here_cols].astype(F32)
            sigmoid = jax.nn.sigmoid(gate)
            silu = gate * sigmoid
            act[block, here_cols] = (silu * up).astype(BF16)
            grads[block, up_cols] = (grad * silu).astype(BF16)
            grads[block, here_cols] = (
                grad * up * sigmoid * (1.0 + gate * (1.0 - sigmoid))
            ).astype(BF16)

        loop(0, hidden // cols, column)

    def pass_on(hop):
        @pl.when(hop > 0)
        def _():
            gather.arrive(hop)

        gather.each(hop, forward)

    loop(0, count, pass_on)

    def term(index, store):
        block = span(index, rows)

        def column(k):
            store(span(k, tile), matmul(grads[block, :], gate_up[span(k, tile), :], NT))

        loop(0, width // tile, column)

    def part(index):
        def store(columns, value):
            going[index, :, columns] = value.astype(BF16)

        term(index, store)

    def own_term(columns, value):
        grad_mid[:, columns] = value

    def put(slot, target):
        return pltpu.make_async_copy(stage.at[slot], target, stores.at[slot])

    def stream(total, compute, target):
        def body(index):
            slot = index % 2

            @pl.when(index >= 2)
            def _():
                put(slot, target(index - 2)).wait()

            stage[slot] = compute(index).astype(BF16)
            put(slot, target(index)).start()

        loop(0, total, body)
        for index in range(max(0, total - 2), total):
            put(index % 2, target(index)).wait()

    across = width // tile

    def output_tile(index):
        return matmul(
            act[span(index // across, tile), :], down_t[span(index % across, tile), :], NT
        )

    def output_target(index):
        return out_part.at[span(index // across, tile), span(index % across, tile)]

    wide = hidden // cols

    def down_tile(index):
        return matmul(cot[:, span(index // wide, tile)], act[:, span(index % wide, cols)], TN)

    def down_target(index):
        columns = pl.ds(pl.multiple_of((2 * wide + index % wide) * cols, cols), cols)
        return weight_grad.at[span(index // wide, tile), columns]

    def gate_up_tile(index):
        return matmul(
            full[:, span(index // (2 * wide), tile)], grads[:, span(index % (2 * wide), cols)], TN
        )

    def gate_up_target(index):
        return weight_grad.at[span(index // (2 * wide), tile), span(index % (2 * wide), cols)]

    def scatter_hop(hop):
        scatter.each(hop, part)
        scatter.step(hop)

        @pl.when(hop == 0)
        def _():
            term(here, own_term)
            stream(count * rows // tile * across, output_tile, output_target)

        @pl.when(hop == 1)
        def _():
            stream(across * wide, down_tile, down_target)

    loop(0, count - 1, scatter_hop)
    stream(across * 2 * wide, gate_up_tile, gate_up_target)
    scatter.finish(grad_mid)
    gather.finish()

    def store_grad(block, value):
        rows_here = pl.ds(here * rows + block.start, block.size)
        grad_mid[block, :] = cot[rows_here, :].astype(F32) + value

    norm_rows_backward(grad_mid, mid_ref, gain_ref, gain_grad, store_grad)


def feed_forward(mid, gain, cot_full, gate_up, down_t, collective):
    count = lax.axis_size("tensor")
    rows, width = mid.shape
    hidden = down_t.shape[1]
    everything = count * rows
    return pl.pallas_call(
        functools.partial(ffn_kernel, count),
        out_shape=[
            jax.ShapeDtypeStruct((rows, width), F32),
            jax.ShapeDtypeStruct((1, width), F32),
            jax.ShapeDtypeStruct((everything, width), BF16),
            jax.ShapeDtypeStruct((width, 3 * hidden), BF16),
        ],
        in_specs=[IN_VMEM, IN_VMEM, IN_HBM, IN_HBM, IN_HBM],
        out_specs=[IN_VMEM, IN_VMEM, IN_HBM, IN_HBM],
        scratch_shapes=gather_scratch(count, rows, width)
        + scatter_scratch(count, rows, width)
        + [
            pltpu.VMEM((everything, width), BF16),
            pltpu.VMEM(gate_up.shape, BF16),
            pltpu.VMEM(down_t.shape, BF16),
            pltpu.VMEM((everything, hidden), BF16),
            pltpu.VMEM((everything, 2 * hidden), BF16),
            pltpu.VMEM((2, tile_of(width), tile_of(hidden)), BF16),
            DMA((3,)),
            DMA((2,)),
        ],
        compiler_params=params(collective),
        cost_estimate=pl.CostEstimate(
            flops=18 * everything * width * hidden,
            transcendentals=everything * hidden,
            bytes_accessed=160 * everything * width,
        ),
        name="feed_forward",
    )(mid, gain[None], cot_full, gate_up, down_t)


def residual_kernel(
    count, grad_ref, mid_ref, part_hbm, weights_hbm, attended,
    hidden_out, grad_attended, weight_grad,
    full, gather_sems, came, going, scatter_sems, total, out_t, loads, out_loads,
):
    here = lax.axis_index("tensor")
    rows, width = mid_ref.shape
    tile = tile_of(width)
    greet_line(here, count)
    out_columns = pl.ds(weights_hbm.shape[1] - out_t.shape[1], out_t.shape[1])
    get_out = pltpu.make_async_copy(weights_hbm.at[:, out_columns], out_t, out_loads.at[0])
    get_out.start()
    full[span(here, rows), :] = grad_ref[...].astype(BF16)

    def fetch(index):
        return pltpu.make_async_copy(
            part_hbm.at[span(index, rows)], going.at[index], loads.at[index]
        )

    loop(0, count, lambda index: fetch(index).start())
    gather = LineGather(here, count, rows, full, gather_sems)
    scatter = LineScatter(here, count, came, going, scatter_sems)
    meet_line(here, count)
    gather.begin()
    loop(0, count, lambda index: fetch(index).wait())
    scatter.step(0)
    total[...] = mid_ref[...] + going[here].astype(F32)

    def backward(index):
        block = span(index, rows)
        grad_attended[block, :] = matmul(full[block, :], out_t[...], NN).astype(BF16)

    get_out.wait()
    gather.each(0, backward)

    def pass_on(hop):
        gather.arrive(hop)

        @pl.when(hop < count - 1)
        def _():
            scatter.step(hop)

        gather.each(hop, backward)

    loop(1, count, pass_on)

    def column(k):
        out_t[span(k, tile), :] = matmul(full[:, span(k, tile)], attended[...], TN).astype(BF16)

    loop(0, width // tile, column)
    put_out = pltpu.make_async_copy(out_t, weight_grad.at[:, out_columns], out_loads.at[0])
    put_out.start()
    scatter.finish(total)
    gather.finish()
    hidden_out[...] = total[...].astype(BF16)
    put_out.wait()


def residual_gather(grad_mid, mid, out_part, weights, attended, collective):
    count = lax.axis_size("tensor")
    rows, width = mid.shape
    return pl.pallas_call(
        functools.partial(residual_kernel, count),
        out_shape=[
            jax.ShapeDtypeStruct((rows, width), BF16),
            jax.ShapeDtypeStruct(attended.shape, BF16),
            jax.ShapeDtypeStruct(weights.shape, BF16),
        ],
        in_specs=[IN_VMEM, IN_VMEM, IN_HBM, IN_HBM, IN_VMEM],
        out_specs=[IN_VMEM, IN_VMEM, IN_HBM],
        scratch_shapes=gather_scratch(count, rows, width)
        + scatter_scratch(count, rows, width)
        + [
            pltpu.VMEM((rows, width), F32),
            pltpu.VMEM((width, attended.shape[1]), BF16),
            DMA((count,)),
            DMA((1,)),
        ],
        compiler_params=params(collective),
        cost_estimate=pl.CostEstimate(
            flops=4 * count * rows * width * attended.shape[1],
            transcendentals=0,
            bytes_accessed=80 * count * rows * width,
        ),
        name="residual_gather",
    )(grad_mid, mid, out_part, weights, attended)


def last_kernel(
    count, grads, weights, hidden_ref, gain_ref, grad_mid, hidden_grad, gain_grad,
    came, going, scatter_sems, total,
):
    here = lax.axis_index("tensor")
    rows, width = hidden_ref.shape
    tile = tile_of(width)
    greet_line(here, count)

    def term(index, store):
        left = grads[span(index, rows), :]

        def column(k):
            store(span(k, tile), matmul(left, weights[span(k, tile), : left.shape[1]], NT))

        loop(0, width // tile, column)

    def part(index):
        def store(columns, value):
            going[index, :, columns] = value.astype(BF16)

        term(index, store)

    def own_term(columns, value):
        total[:, columns] = value

    scatter = LineScatter(here, count, came, going, scatter_sems)
    scatter.each(0, part)
    meet_line(here, count)
    scatter.step(0)
    term(here, own_term)

    def scatter_hop(hop):
        scatter.each(hop, part)
        scatter.step(hop)

    loop(1, count - 1, scatter_hop)
    scatter.finish(total)

    def store_grad(block, value):
        hidden_grad[block, :] = (grad_mid[block, :] + value).astype(BF16)

    norm_rows_backward(total, hidden_ref, gain_ref, gain_grad, store_grad)


def last_scatter(grads, weights, hidden, gain, grad_mid, collective):
    count = lax.axis_size("tensor")
    rows, width = hidden.shape
    return pl.pallas_call(
        functools.partial(last_kernel, count),
        out_shape=[
            jax.ShapeDtypeStruct((rows, width), BF16),
            jax.ShapeDtypeStruct((1, width), F32),
        ],
        in_specs=[IN_VMEM] * 5,
        out_specs=[IN_VMEM] * 2,
        scratch_shapes=scatter_scratch(count, rows, width) + [pltpu.VMEM((rows, width), F32)],
        compiler_params=params(collective),
        cost_estimate=pl.CostEstimate(
            flops=0, transcendentals=0, bytes_accessed=64 * count * rows * width
        ),
        name="last_scatter",
    )(grads, weights, hidden, gain[None], grad_mid)


def rope_of(values, cosine, signed_sine):
    return values * cosine + pltpu.roll(values, HEAD_DIM // 2, 1) * signed_sine


def rope_back(grad, cosine, signed_sine):
    return grad * cosine - pltpu.roll(grad, HEAD_DIM // 2, 1) * signed_sine


def head_columns(index):
    return pl.ds(pl.multiple_of(index * HEAD_DIM, HEAD_DIM), HEAD_DIM)


def attention_kernel(
    heads, kv_heads, sequence, normed_hbm, weights_hbm, cosine, signed_sine, query_gain, key_gain,
    raw, rotated, attended, normed, weights, loads,
):
    rows = normed.shape[0]
    width = (heads + 2 * kv_heads) * HEAD_DIM
    block = math.gcd(rows, 256)
    get_weights = pltpu.make_async_copy(weights_hbm.at[:, pl.ds(0, width)], weights, loads.at[0])
    get_normed = pltpu.make_async_copy(normed_hbm, normed, loads.at[1])
    get_weights.start()
    get_normed.start()
    get_weights.wait()
    get_normed.wait()
    positions = sequence // block

    def project(index):
        here = span(index, block)
        table = span(index % positions, block)
        cos, sin = cosine[table, :], signed_sine[table, :]
        left = normed[here, :]
        groups = 4 if (heads + kv_heads) % 4 == 0 and (2 * kv_heads) % 4 == 0 else 1
        for first in range(0, heads + 2 * kv_heads, groups):
            several = slice(first * HEAD_DIM, (first + groups) * HEAD_DIM)
            made = matmul(left, weights[:, several], NN)
            for k in range(groups):
                head = first + k
                columns = slice(head * HEAD_DIM, (head + 1) * HEAD_DIM)
                value = made[:, k * HEAD_DIM : (k + 1) * HEAD_DIM]
                if head < heads + kv_heads:
                    raw[here, columns] = value
                    gain = query_gain if head < heads else key_gain
                    inverse = lax.rsqrt(
                        jnp.mean(value * value, axis=-1, keepdims=True) + EPSILON
                    )
                    value = rope_of(value * inverse * gain[...], cos, sin)
                rotated[here, columns] = value.astype(BF16)

    loop(0, rows // block, project)
    scale = 1.0 / math.sqrt(HEAD_DIM)

    def one_head(index):
        start, head = (index // heads) * sequence, index % heads
        kv = head // (heads // kv_heads)
        for k in range(positions):
            length = (k + 1) * block
            here = pl.ds(pl.multiple_of(start + k * block, block), block)
            keys = pl.ds(pl.multiple_of(start, block), length)
            query = rotated[here, head_columns(head)]
            scores = matmul(query, rotated[keys, head_columns(heads + kv)], NT) * scale
            at_row = lax.broadcasted_iota(jnp.int32, scores.shape, 0) + k * block
            at_column = lax.broadcasted_iota(jnp.int32, scores.shape, 1)
            scores = jnp.where(at_column <= at_row, scores, NEG_FILL)
            powers = jnp.exp(scores - jnp.max(scores, axis=-1, keepdims=True))
            probs = powers * (1.0 / jnp.sum(powers, axis=-1, keepdims=True))
            attended[here, head_columns(head)] = matmul(
                probs.astype(BF16), rotated[keys, head_columns(heads + kv_heads + kv)], NN
            ).astype(BF16)

    loop(0, (rows // sequence) * heads, one_head)


def attention_forward(normed, weights, tables, gains, heads, kv_heads):
    rows, width = normed.shape
    across = (heads + 2 * kv_heads) * HEAD_DIM
    return pl.pallas_call(
        functools.partial(attention_kernel, heads, kv_heads, SEQ_LEN),
        out_shape=[
            jax.ShapeDtypeStruct((rows, (heads + kv_heads) * HEAD_DIM), F32),
            jax.ShapeDtypeStruct((rows, across), BF16),
            jax.ShapeDtypeStruct((rows, heads * HEAD_DIM), BF16),
        ],
        in_specs=[IN_HBM] * 2 + [IN_VMEM] * 4,
        out_specs=[IN_VMEM] * 3,
        scratch_shapes=[
            pltpu.VMEM((rows, width), BF16),
            pltpu.VMEM((width, across), BF16),
            DMA((2,)),
        ],
        compiler_params=params(),
        cost_estimate=pl.CostEstimate(
            flops=2 * rows * width * across,
            transcendentals=rows * SEQ_LEN * heads,
            bytes_accessed=20 * rows * width,
        ),
        name="attention_forward",
    )(normed, weights, *tables, *gains)


def attention_back_kernel(
    heads, kv_heads, sequence, normed_hbm, raw, rotated, attended, grad_attended,
    cosine, signed_sine, query_gain, key_gain, given,
    grads, weight_grad, gain_grad,
    normed, grad_rot, stage, loads, stores,
):
    rows = normed.shape[0]
    block = math.gcd(rows, 256)
    positions = sequence // block
    get_normed = pltpu.make_async_copy(normed_hbm, normed, loads.at[0])
    get_normed.start()
    scale = 1.0 / math.sqrt(HEAD_DIM)
    grad_rot[:, heads * HEAD_DIM :] = jnp.zeros_like(grad_rot[:, heads * HEAD_DIM :])

    def one_head(index):
        start, head = (index // heads) * sequence, index % heads
        kv = head // (heads // kv_heads)
        key_columns, value_columns = head_columns(heads + kv), head_columns(heads + kv_heads + kv)
        for k in range(positions):
            length = (k + 1) * block
            here = pl.ds(pl.multiple_of(start + k * block, block), block)
            keys = pl.ds(pl.multiple_of(start, block), length)
            query, key = rotated[here, head_columns(head)], rotated[keys, key_columns]
            grad = grad_attended[here, head_columns(head)]
            scores = matmul(key, query, NT) * scale
            at_key = lax.broadcasted_iota(jnp.int32, scores.shape, 0)
            at_query = lax.broadcasted_iota(jnp.int32, scores.shape, 1) + k * block
            scores = jnp.where(at_key <= at_query, scores, NEG_FILL)
            powers = jnp.exp(scores - jnp.max(scores, axis=0, keepdims=True))
            probs = powers * (1.0 / jnp.sum(powers, axis=0, keepdims=True))
            product = grad.astype(F32) * attended[here, head_columns(head)].astype(F32)
            delta = jnp.sum(jnp.transpose(product), axis=0, keepdims=True)
            grad_rot[keys, value_columns] += matmul(probs.astype(BF16), grad, NN)
            grad_probs = matmul(rotated[keys, value_columns], grad, NT)
            grad_scores = (probs * (grad_probs - delta) * scale).astype(BF16)
            grad_rot[keys, key_columns] += matmul(grad_scores, query, NN)
            grad_rot[here, head_columns(head)] = matmul(grad_scores, key, TN)

    loop(0, (rows // sequence) * heads, one_head)
    gain_grad[...] = jnp.zeros_like(gain_grad)

    def unrotate(index):
        here = span(index, block)
        table = span(index % positions, block)
        cos, sin = cosine[table, :], signed_sine[table, :]
        for head in range(heads + 2 * kv_heads):
            columns = slice(head * HEAD_DIM, (head + 1) * HEAD_DIM)
            grad = grad_rot[here, columns]
            if head < heads + kv_heads:
                which = 0 if head < heads else 1
                gain = query_gain if head < heads else key_gain
                grad = rope_back(grad, cos, sin)
                value = raw[here, columns]
                inverse = lax.rsqrt(jnp.mean(value * value, axis=-1, keepdims=True) + EPSILON)
                unit = value * inverse
                gain_grad[which : which + 1, :] += jnp.sum(grad * unit, axis=0, keepdims=True)
                grad_unit = grad * gain[...]
                mean = jnp.mean(grad_unit * unit, axis=-1, keepdims=True)
                grad = inverse * (grad_unit - unit * mean)
            grads[here, columns] = grad.astype(BF16)

    loop(0, rows // block, unrotate)
    get_normed.wait()
    tile, cols = stage.shape[1:]
    wide = grads.shape[1] // cols

    def target(index):
        return weight_grad.at[span(index // wide, tile), span(index % wide, cols)]

    def put(index):
        return pltpu.make_async_copy(stage.at[index % 2], target(index), stores.at[index % 2])

    total = normed.shape[1] // tile * wide

    def weight_tile(index):
        @pl.when(index >= 2)
        def _():
            put(index - 2).wait()

        left, right = normed[:, span(index // wide, tile)], grads[:, span(index % wide, cols)]
        stage[index % 2] = matmul(left, right, TN).astype(BF16)
        put(index).start()

    loop(0, total, weight_tile)
    for index in range(max(0, total - 2), total):
        put(index).wait()


def attention_backward(normed, raw, rotated, attended, grad_attended, tables, gains, weight_grad, heads, kv_heads):
    rows, width = normed.shape
    across = (heads + 2 * kv_heads) * HEAD_DIM
    return pl.pallas_call(
        functools.partial(attention_back_kernel, heads, kv_heads, SEQ_LEN),
        out_shape=[
            jax.ShapeDtypeStruct((rows, across), BF16),
            jax.ShapeDtypeStruct(weight_grad.shape, BF16),
            jax.ShapeDtypeStruct((2, HEAD_DIM), F32),
        ],
        in_specs=[IN_HBM] + [IN_VMEM] * 8 + [IN_HBM],
        out_specs=[IN_VMEM, IN_HBM, IN_VMEM],
        input_output_aliases={9: 1},
        scratch_shapes=[
            pltpu.VMEM((rows, width), BF16),
            pltpu.VMEM((rows, across), F32),
            pltpu.VMEM((2, tile_of(width), tile_of(across)), BF16),
            DMA((1,)),
            DMA((2,)),
        ],
        compiler_params=params(),
        cost_estimate=pl.CostEstimate(
            flops=4 * rows * width * across,
            transcendentals=rows * SEQ_LEN * heads,
            bytes_accessed=30 * rows * width,
        ),
        name="attention_backward",
    )(normed, raw, rotated, attended, grad_attended, *tables, *gains, weight_grad)


def total_kernel(line, planes, x_ref, out_ref, slots, send, recv):
    plane, here = lax.axis_index("dp"), lax.axis_index("tensor")
    me, everyone = plane * line + here, line * planes
    barrier = pltpu.get_barrier_semaphore()

    def greet(index, carry):
        @pl.when(index != me)
        def _():
            pl.semaphore_signal(
                barrier, inc=1, device_id=(index // line, index % line), device_id_type=MESH
            )

        return carry

    lax.fori_loop(0, everyone, greet, 0)
    pl.semaphore_wait(barrier, everyone - 1)

    def to(index):
        return pltpu.make_async_remote_copy(
            src_ref=x_ref,
            dst_ref=slots.at[me],
            send_sem=send.at[index],
            recv_sem=recv.at[me],
            device_id=(index // line, index % line),
            device_id_type=MESH,
        )

    def came(index):
        return pltpu.make_async_remote_copy(
            src_ref=x_ref,
            dst_ref=slots.at[index],
            send_sem=send.at[index],
            recv_sem=recv.at[index],
            device_id=(index // line, index % line),
            device_id_type=MESH,
        )

    def push(index, carry):
        @pl.when(index != me)
        def _():
            to(index).start()

        return carry

    lax.fori_loop(0, everyone, push, 0)
    slots[me] = x_ref[...]

    def settle(index, carry):
        @pl.when(index != me)
        def _():
            came(index).wait_recv()
            to(index).wait_send()

        return carry

    lax.fori_loop(0, everyone, settle, 0)

    def add(index, total):
        return total + slots[index]

    out_ref[...] = lax.fori_loop(0, everyone, add, jnp.zeros(x_ref.shape, jnp.float32))


def total_over_all(x, collective):
    line, planes = lax.axis_size("tensor"), lax.axis_size("dp")
    return pl.pallas_call(
        functools.partial(total_kernel, line, planes),
        out_shape=jax.ShapeDtypeStruct(x.shape, x.dtype),
        in_specs=[pl.BlockSpec(memory_space=pltpu.VMEM)],
        out_specs=pl.BlockSpec(memory_space=pltpu.VMEM),
        scratch_shapes=[
            pltpu.VMEM((line * planes,) + x.shape, x.dtype),
            pltpu.SemaphoreType.DMA((line * planes,)),
            pltpu.SemaphoreType.DMA((line * planes,)),
        ],
        compiler_params=pltpu.CompilerParams(collective_id=collective, has_side_effects=True),
    )(x)


def rope_tables(positions, width):
    half_width = width // 2
    freqs = ROPE_BASE ** (-(jnp.arange(half_width, dtype=F32) * (2.0 / width)))
    angles = positions.astype(F32)[:, None] * freqs[None, :]
    cosine, sine = jnp.cos(angles), jnp.sin(angles)
    return (
        jnp.concatenate([cosine, cosine], axis=1),
        jnp.concatenate([-sine, sine], axis=1),
    )


def per_device(
    hidden_in,
    query_proj,
    key_proj,
    value_proj,
    out_proj,
    gate_proj,
    up_proj,
    down_proj,
    attn_norm,
    query_norm,
    key_norm,
    ffn_norm,
    cotangent,
):
    heads_width, kv_width = query_proj.shape[1], key_proj.shape[1]
    heads, kv_heads = heads_width // HEAD_DIM, kv_width // HEAD_DIM
    qkv_width = heads_width + 2 * kv_width
    attn_full = lax.all_gather(
        jnp.concatenate([query_proj, key_proj, value_proj, out_proj.T], axis=1),
        "dp",
        axis=0,
        tiled=True,
    )
    normed = first_gather(hidden_in, attn_norm, 0)
    down_full_t = lax.all_gather(down_proj.T, "dp", axis=0, tiled=True)
    gate_up_full = lax.all_gather(
        jnp.concatenate([gate_proj, up_proj], axis=1), "dp", axis=0, tiled=True
    )
    tables = rope_tables(jnp.arange(SEQ_LEN), HEAD_DIM)
    gains = (query_norm[None], key_norm[None])
    raw, rotated, attended = attention_forward(normed, attn_full, tables, gains, heads, kv_heads)
    residual_mid, cot_full = middle_scatter(attended, attn_full, hidden_in, cotangent, 1)
    grad_mid, ffn_gain_grad, out_part, ffn_grads = feed_forward(
        residual_mid, ffn_norm, cot_full, gate_up_full, down_full_t, 2
    )

    def scatter(parts):
        return lax.psum_scatter(parts, "dp", scatter_dimension=0, tiled=True)

    ffn_sums = scatter(ffn_grads)
    hidden_out, grad_attended, attn_grads = residual_gather(
        grad_mid, residual_mid, out_part, attn_full, attended, 3
    )
    grads, attn_grads, head_gain_grads = attention_backward(
        normed, raw, rotated, attended, grad_attended, tables, gains, attn_grads, heads, kv_heads
    )
    attn_grads, ffn_sums = lax.optimization_barrier((attn_grads, ffn_sums))
    attn_sums = scatter(attn_grads)
    dhidden_in, attn_gain_grad = last_scatter(grads, attn_full, hidden_in, attn_norm, grad_mid, 4)
    parts = (attn_gain_grad, ffn_gain_grad, head_gain_grads)
    packed = jnp.concatenate([part.reshape(-1, HEAD_DIM) for part in parts])
    gain_total = total_over_all(packed, 5)
    cut = attn_norm.shape[0] // HEAD_DIM
    gate_sum, up_sum, down_sum_t = jnp.split(ffn_sums.astype(F32), 3, axis=1)
    query_sum, key_sum, value_sum, out_sum_t = jnp.split(
        attn_sums.astype(F32), [heads_width, heads_width + kv_width, qkv_width], axis=1
    )
    return (
        hidden_out,
        dhidden_in,
        query_sum,
        key_sum,
        value_sum,
        out_sum_t.T,
        gate_sum,
        up_sum,
        down_sum_t.T,
        gain_total[:cut].reshape(-1),
        gain_total[2 * cut],
        gain_total[2 * cut + 1],
        gain_total[cut : 2 * cut].reshape(-1),
    )


def solution(mesh):
    placed = (
        P(("dp", "tensor"), None),
        P("dp", "tensor"),
        P("dp", "tensor"),
        P("dp", "tensor"),
        P("tensor", "dp"),
        P("dp", "tensor"),
        P("dp", "tensor"),
        P("tensor", "dp"),
        P(),
        P(),
        P(),
        P(),
        P(("dp", "tensor"), None),
    )
    return jax.shard_map(
        per_device,
        mesh=mesh,
        in_specs=placed,
        out_specs=(
            P(("dp", "tensor"), None),
            P(("dp", "tensor"), None),
            P("dp", "tensor"),
            P("dp", "tensor"),
            P("dp", "tensor"),
            P("tensor", "dp"),
            P("dp", "tensor"),
            P("dp", "tensor"),
            P("tensor", "dp"),
            P(),
            P(),
            P(),
            P(),
        ),
        check_vma=False,
    )
```

time: 895 us -> 637 us (0.71); the launches traced: 879 us -> 633 us
  matrix products: 175 us -> 0 us
  other arithmetic: 69.8 us -> 11.6 us
  local copies, waits for them, and re-layouts: 30.7 us -> 16.1 us
    dot_general x33 -> x0, matrix products: 175 us -> none  [the longest x4 30.9 us: matmul(): lax.dot_general(left, right, (dims, ((), ())), preferred_element_type=jnp...]
    concatenate x6 -> x2, other arithmetic: 31.8 us -> 2.62 us  [the longest x1 1.31 us: rope_tables(): jnp.concatenate([cosine, cosine], axis=1)]
    unnamed x162 -> x24, local copies, waits for them, and re-layouts: 22.6 us -> 8.46 us
    reduce_sum x10 -> x0, other arithmetic: 14 us -> none  [the longest x5 7.03 us: norm_backward(): jnp.sum((grad_normed * unit_vals).reshape(-1, gain.shape[0]), axis=0)]
    pallas_call x8 -> x7, Pallas kernels: 565 us -> 566 us  [the longest x1 149 us: feed_forward(): pl.pallas_call(functools.partial(ffn_kernel, count), out_shape=[jax.Shape...]
  transfers between devices with their start and end apart: 6 -> 5, of which waited for: 0 -> 1; matrix products, arithmetic and copies ran while one was open for 16% -> 3% of each run, Pallas kernels for 51% -> 69%
where the time goes in v2:
time: 637 us; the launch traced here: 633 us
  Pallas kernels  584 us (92%)
  local copies, waits for them, and re-layouts  16.1 us (3%)
  between operations  14 us (2%)
  other arithmetic  11.6 us (2%)
  waiting for transfers between devices  7.06 us (1%)
    pallas_call x1, Pallas kernels, feed_forward(): pl.pallas_call(functools.partial(ffn_kernel, count), out_shape=[jax.Shape...  149 us
    pallas_call x1, Pallas kernels, middle_scatter(): pl.pallas_call(functools.partial(middle_kernel, count), out_shape=[jax.Sh...  119 us
    pallas_call x1, Pallas kernels, residual_gather(): pl.pallas_call(functools.partial(residual_kernel, count), out_shape=[jax....  91.8 us
    pallas_call x1, Pallas kernels, last_scatter(): pl.pallas_call(functools.partial(last_kernel, count), out_shape=[jax.Shap...  78.3 us
    pallas_call x1, Pallas kernels, first_gather(): pl.pallas_call(functools.partial(first_kernel, count), out_shape=jax.Shap...  71.1 us
    pallas_call x1, Pallas kernels, attention_backward(): pl.pallas_call(functools.partial(attention_back_kernel, heads, kv_heads,...  31.5 us
    pallas_call x1, Pallas kernels, attention_forward(): pl.pallas_call(functools.partial(attention_kernel, heads, kv_heads, SEQ_L...  25.7 us
    pallas_call x1, Pallas kernels, total_over_all(): pl.pallas_call(functools.partial(total_kernel, line, planes), out_shape=j...  18 us
  transfers between devices with their start and end apart: 5, of which 1 were waited for; matrix products, arithmetic and copies ran while one was open for 3% of the time, Pallas kernels for 69%

profile of v2, /device:TPU:9, one launch (start us, length us, event | category | flops | bytes accessed | tf_op | source)
XLA Modules:
  0.0 633.0 jit_solution(9535998309765555771)
XLA Ops:
  7.2 1.2 copy.27
  8.4 2.1 pad_maximum_fusion.1
  10.6 1.2 copy.28
  11.9 1.4 pad_maximum_fusion
  13.3 71.1 %first_gather.1.normed_hbm = bf16[1024,2048]{1,0:T(8,128)(2,1)} custom-call(bf16[256,2048]{1,0:T(8,128)(2,1)} %hidden_ref.5, f32[1,2048]{1,0:T(1,128)} %bitcast.22), custom_call_target="tpu_custom_call" | custom-call | bytes 134217728 | tf_op jit(solution)/shard_map/first_gather/pallas_call | solution.py:323
  84.4 1.9 fusion
  86.3 1.3 pad_maximum_fusion.2
  87.6 25.7 %attention_forward.1 = (f32[1024,768]{1,0:T(8,128)}, bf16[1024,1024]{1,0:T(8,128)(2,1)}, bf16[1024,512]{1,0:T(8,128)(2,1)}) custom-call(bf16[1024,2048]{1,0:T(8,128)(2,1)} %first_gather.1.normed_hbm, bf16[2048,1536]{1,0:T(8,128)(2,1)} %all-gather.4.cloned.1.call-done.weights_hbm.weights, f32[1024,128]{1,0:T(8,128)} %get-tuple-element.75.cosine, ...), custom_call_target="tpu_custom_call" | custom-call | flops 4294967296 | bytes 41943040 | tf_op jit(solution)/shard_map/attention_forward/pallas_call | solution.py:843
  113.4 118.7 %middle_scatter.1 = (f32[256,2048]{1,0:T(8,128)}, bf16[1024,2048]{1,0:T(8,128)(2,1)}) custom-call(bf16[1024,512]{1,0:T(8,128)(2,1)} %get-tuple-element.32.attended, bf16[2048,1536]{1,0:T(8,128)(2,1)} %all-gather.4.cloned.1.call-done.weights_hbm.weights, bf16[256,2048]{1,0:T(8,128)(2,1)} %hidden_ref.5, bf16[256,2048]{1,0:T(8,128)(2,1)} %cot_ref.1), custom_call_target="tpu_custom_call" | custom-call | bytes 167772160 | tf_op jit(solution)/shard_map/middle_scatter/pallas_call | solution.py:405
  232.1 148.9 %feed_forward.1 = (f32[256,2048]{1,0:T(8,128)}, f32[1,2048]{1,0:T(1,128)}, bf16[1024,2048]{1,0:T(8,128)(2,1)}, bf16[2048,4608]{1,0:T(8,128)(2,1)}) custom-call(f32[256,2048]{1,0:T(8,128)} %get-tuple-element.33.mid_ref, f32[1,2048]{1,0:T(1,128)} %bitcast.26, bf16[1024,2048]{1,0:T(8,128)(2,1)} %get-tuple-element.34.cot_hbm, ...), custom_call_target="tpu_custom_call" | custom-call | flops 57982058496 | bytes 335544320 | tf_op jit(solution)/shard_map/feed_forward/pallas_call | solution.py:582
  381.1 91.8 %residual_gather.1 = (bf16[256,2048]{1,0:T(8,128)(2,1)}, bf16[1024,512]{1,0:T(8,128)(2,1)}, bf16[2048,1536]{1,0:T(8,128)(2,1)}) custom-call(f32[256,2048]{1,0:T(8,128)} %get-tuple-element.35.grad_ref.grad_mid, f32[256,2048]{1,0:T(8,128)} %get-tuple-element.33.mid_ref, bf16[1024,2048]{1,0:T(8,128)(2,1)} %get-tuple-element.36.part_hbm, ...), custom_call_target="tpu_custom_call" | custom-call | flops 4294967296 | bytes 167772160 | tf_op jit(solution)/shard_map/residual_gather/pallas_call | solution.py:675
  473.0 31.5 %attention_backward.1 = (bf16[1024,1024]{1,0:T(8,128)(2,1)}, bf16[2048,1536]{1,0:T(8,128)(2,1)}, f32[2,128]{1,0:T(2,128)}) custom-call(bf16[1024,2048]{1,0:T(8,128)(2,1)} %first_gather.1.normed_hbm, f32[1024,768]{1,0:T(8,128)} %get-tuple-element.38.raw, bf16[1024,1024]{1,0:T(8,128)(2,1)} %get-tuple-element.39.rotated, ...), custom_call_target="tpu_custom_call", output_to_operand_aliasing={{1}: (9, {})} | custom-call | flops 8589934592 | bytes 62914560 | tf_op jit(solution)/shard_map/attention_backward/pallas_call | solution.py:958
  504.5 6.9 %reduce-scatter.3.cloned.1.call-done = bf16[256,4608]{1,0:T(8,128)(2,1)} async-done(((bf16[2048,4608]{1,0:T(8,128)(2,1)}), bf16[256,4608]{1,0:T(8,128)(2,1)}) %reduce-scatter.3.cloned.1.call-update) | async-done | bytes 2359312 | tf_op jit(solution)/shard_map/reduce_scatter | solution.py:1113
  511.5 78.3 %last_scatter.1 = (bf16[256,2048]{1,0:T(8,128)(2,1)}, f32[1,2048]{1,0:T(1,128)}) custom-call(bf16[1024,1024]{1,0:T(8,128)(2,1)} %get-tuple-element.42.grads, bf16[2048,1536]{1,0:T(8,128)(2,1)} %all-gather.4.cloned.1.call-done.weights_hbm.weights, bf16[256,2048]{1,0:T(8,128)(2,1)} %hidden_ref.5, f32[1,2048]{1,0:T(1,128)} %bitcast.23, ...), custom_call_target="tpu_custom_call" | custom-call | bytes 134217728 | tf_op jit(solution)/shard_map/last_scatter/pallas_call | solution.py:750
  589.8 1.3 pad_maximum_fusion.4.x_ref
  591.1 18.0 %shard_map.228 = f32[34,128]{1,0:T(8,128)} custom-call(f32[34,128]{1,0:T(8,128)} %pad_maximum_fusion.4.x_ref), custom_call_target="tpu_custom_call" | custom-call | tf_op jit(solution)/shard_map/pallas_call | solution.py:1050
  609.1 1.3 slice_bitcast_fusion.4
  610.4 1.3 slice_bitcast_fusion.2
  611.7 2.2 convert_element_type.21
  613.9 1.3 slice_bitcast_fusion
  615.2 3.2 copy.30
  618.4 2.1 fusion.1
  620.4 1.4 convert_element_type.20
  621.9 1.0 copy.29
  (39 shorter events, 4.0 us)
Async XLA Ops:
  7.2 3.4 copy-start.4
  7.2 80.4 %all-gather.4.cloned.1.call-start = ((), (), s32[]{:S(2)}) async-start(), calls=%async_computation.2 | async-start | bytes 7077888 | tf_op jit(solution)/shard_map/all_gather | solution.py:1093
  8.4 3.5 copy-start.5
  8.4 3.5 copy-start.6
  10.6 221.5 %all-gather.8.cloned.1.call-start = ((), (), s32[]{:S(2)}) async-start(), calls=%async_computation.4 | async-start | bytes 7077888 | tf_op jit(solution)/shard_map/all_gather | solution.py:1100
  11.8 220.3 %all-gather.6.cloned.1.call-start = ((), (), s32[]{:S(2)}) async-start(), calls=%async_computation.3 | async-start | bytes 14155776 | tf_op jit(solution)/shard_map/all_gather | solution.py:1101
  13.3 498.2 %reduce-scatter.3.cloned.1.call-start = ((), (), s32[]{:S(2)}) async-start(), calls=%async_computation.5 | async-start | bytes 21233664 | tf_op jit(solution)/shard_map/reduce_scatter | solution.py:1113
  381.1 239.3 %reduce-scatter.5.cloned.1.call-start = ((), (), s32[]{:S(2)}) async-start(), calls=%async_computation.6 | async-start | bytes 7077888 | tf_op jit(solution)/shard_map/reduce_scatter | solution.py:1113
  511.5 78.3 %copy-start.7 = (f32[1,2048]{1,0:T(1,128)S(1)}, f32[1,2048]{1,0:T(1,128)}, u32[]{:S(2)}) copy-start(f32[1,2048]{1,0:T(1,128)} %get-tuple-element.49) | copy-start | bytes 24580
  511.5 78.3 %copy-start.8 = (f32[2,128]{1,0:T(2,128)S(1)}, f32[2,128]{1,0:T(2,128)}, u32[]{:S(2)}) copy-start(f32[2,128]{1,0:T(2,128)} %get-tuple-element.50) | copy-start | bytes 3076
  615.2 3.2 copy-start
  620.4 2.4 copy-start.1
  621.8 2.7 copy-start.2
  622.9 2.7 copy-start.3
Sparse Core Ops, SparseCore 0:
  10.7 46.9 all-gather.3
  60.1 45.3 all-gather.7
  108.0 72.0 all-gather.5
  381.2 130.1 reduce-scatter.2
  514.7 61.7 reduce-scatter.4
